TPU v7x, 32 devices: a whole 2x2x4 slice. The times are simulated.
32 devices in a mesh: gx: 4 (over x, core), gy: 4 (over z), gz: 2 (over y).
Axes of the slice: x: 2, y: 2, z: 4, core: 2. Of those that a mesh axis runs over, the one named last changes fastest.
Arguments:
- estimate: float32 [32, 64, 512], P('gz', 'gx', 'gy'), may hold values from 0.5 to 2
- measured: float32 [32, 64, 512], P('gz', 'gx', 'gy'), may hold values from 0.1 to 10
- point_spread: float32 [32, 1024], replicated, may hold values from 0.0005 to 4.01, as said below
Outputs:
- updated: float32 [32, 64, 512], P('gz', 'gx', 'gy')
- mip_x: float32 [32, 512], P('gz', 'gy')
- mip_y: float32 [32, 64], P('gz', 'gx')
- mip_z: float32 [64, 512], P('gx', ('gy', 'gz'))
Inputs may be any that keep to these rules, and one draw needn't show every extreme that they name: `point_spread`: every entry is positive.
All inputs are finite; a program needn't handle non-finite values.
Results may differ from a plain program's by a relative error of at most 0.000076.
Values sent between devices are 32-bit elements; how exact they have to be, the bound alone decides.
No kernel may reach another device: no remote copies, remote signals or barrier semaphores. Data moves between devices by JAX's collectives and lax.ppermute only.
A program may use at most 64 MiB of HBM per device.

v0:
```python
import functools

import jax
import jax.numpy as jnp
import numpy as np
from jax import lax
from jax.experimental import pallas as pl
from jax.experimental.pallas import tpu as pltpu
from jax.sharding import PartitionSpec as P

F32 = jnp.float32
BF16 = jnp.bfloat16


def split(value):
    high = value.astype(BF16)
    return high, (value - high.astype(F32)).astype(BF16)


def constant(table):
    table = np.asarray(table, np.float32)
    high = table.astype(BF16)
    low = (table - high.astype(np.float32)).astype(BF16)
    return jnp.asarray(high), jnp.asarray(low)


def dot3(left, right):
    mul = functools.partial(jnp.dot, preferred_element_type=F32)
    return mul(left[0], right[0]) + (mul(left[0], right[1]) + mul(left[1], right[0]))


def angles(rows, cols, length):
    return np.mod(np.outer(rows, cols), length) * (2.0 * np.pi / length)


def forward_left(length, positions):
    theta = angles(np.arange(length), positions, length)
    c, s = np.cos(theta), np.sin(theta)
    return np.block([[c, s], [-s, c]])


def inverse_left(length, positions):
    theta = angles(positions, np.arange(length), length)
    c, s = np.cos(theta), np.sin(theta)
    return np.block([[c, -s], [s, c]])


def forward_right(length, positions, lanes):
    count = length // 2 + 1
    theta = angles(positions, np.arange(count), length)
    out = np.zeros((len(positions), 2 * lanes))
    out[:, :count] = np.cos(theta)
    out[:, lanes : lanes + count] = -np.sin(theta)
    return out


def inverse_right(length, positions, lanes):
    count = length // 2 + 1
    freq = np.arange(count)
    weight = np.where((freq == 0) | (2 * freq == length), 1.0, 2.0)[:, None]
    theta = angles(freq, positions, length)
    out = np.zeros((2 * lanes, len(positions)))
    out[:count] = weight * np.cos(theta)
    out[lanes : lanes + count] = -weight * np.sin(theta)
    return out


def pair_x(s1, row, rows, lanes):
    block = s1[pl.ds(row, rows), :]
    return jnp.concatenate([block[:, :lanes], block[:, lanes:]], axis=0)


def pair_strided(ref, start, gap, rows, stride):
    return jnp.concatenate(
        [ref[pl.ds(start, rows, stride=stride), :], ref[pl.ds(start + gap, rows, stride=stride), :]], axis=0
    )


def transform_x(s1, s2, table, count_z, count_x, length_x, lanes):
    def step(i, carry):
        z = i * 2
        data = jnp.concatenate(
            [pair_x(s1, (z + j) * count_x, count_x, lanes) for j in range(2)], axis=1
        )
        out = dot3(table, split(data))
        for j in range(2):
            s2[pl.ds((z + j) * 2 * length_x, 2 * length_x), :] = out[:, j * lanes : (j + 1) * lanes]
        return carry

    lax.fori_loop(0, count_z // 2, step, 0, unroll=4)


def spectrum_body(psf, ty_h, ty_l, fx_h, fx_l, fz_h, fz_l, spec, s1, s2, *, extent, dims, lanes):
    length_z, length_x, length_y = dims
    values = psf[...]
    scale = 1.0 / (jnp.sum(values) * float(length_z * length_x * length_y))
    s1[...] = dot3(split(values), (ty_h[...], ty_l[...])) * scale
    transform_x(s1, s2, (fx_h[...], fx_l[...]), extent, extent, length_x, lanes)
    table = (fz_h[...], fz_l[...])

    def step(i, carry):
        k = i * 2
        data = jnp.concatenate(
            [pair_strided(s2, k + j, length_x, extent, 2 * length_x) for j in range(2)], axis=1
        )
        out = dot3(table, split(data))
        for j in range(2):
            spec[pl.ds((k + j) * 2 * length_z, 2 * length_z), :] = out[:, j * lanes : (j + 1) * lanes]
        return carry

    lax.fori_loop(0, length_x // 2, step, 0, unroll=4)


def conv_body(
    left, mid, right, own, spec, ty_h, ty_l, fx_h, fx_l, fz_h, fz_l, gz_h, gz_l, gx_h, gx_l, iy_h, iy_l,
    *rest, brick, dims, lanes, groups, conj,
):
    outs, (s1, s2, s3, s4) = rest[:-4], rest[-4:]
    brick_z, brick_x, brick_y = brick
    length_z, length_x, length_y = dims
    rows = brick_z * brick_x
    chunk = rows // groups
    block = rows + chunk
    for g in range(groups):
        table = (ty_h[g], ty_l[g])
        for bx, ref in enumerate((left, mid, right)):
            data = jnp.concatenate(
                [
                    jnp.concatenate(
                        [ref[pl.ds(b * block + g * chunk, chunk), :], ref[pl.ds(b * block + rows, chunk), :]],
                        axis=1,
                    )
                    for b in range(3)
                ],
                axis=0,
            )
            out = dot3(split(data), table)
            per = chunk // brick_x
            for b in range(3):
                for zi in range(per):
                    z = b * brick_z + g * per + zi
                    src = b * chunk + zi * brick_x
                    s1[pl.ds(z * length_x + bx * brick_x, brick_x), :] = out[src : src + brick_x]
    transform_x(s1, s2, (fx_h[...], fx_l[...]), length_z, length_x, length_x, lanes)
    fz = (fz_h[...], fz_l[...])
    gz = (gz_h[...], gz_l[...])

    def middle(i, carry):
        k = i * 2
        data = jnp.concatenate(
            [pair_strided(s2, k + j, length_x, length_z, 2 * length_x) for j in range(2)], axis=1
        )
        out = dot3(fz, split(data))
        kern = jnp.concatenate(
            [spec[pl.ds((k + j) * 2 * length_z, 2 * length_z), :] for j in range(2)], axis=1
        )
        re, im = out[:length_z], out[length_z:]
        kr, ki = kern[:length_z], kern[length_z:]
        if conj:
            prod = jnp.concatenate([re * kr + im * ki, im * kr - re * ki], axis=0)
        else:
            prod = jnp.concatenate([re * kr - im * ki, re * ki + im * kr], axis=0)
        back = dot3(gz, split(prod))
        for j in range(2):
            s3[pl.ds((k + j) * 2 * brick_z, 2 * brick_z), :] = back[:, j * lanes : (j + 1) * lanes]
        return carry

    lax.fori_loop(0, length_x // 2, middle, 0, unroll=4)
    gx = (gx_h[...], gx_l[...])
    for z in range(0, brick_z, 2):
        data = jnp.concatenate(
            [pair_strided(s3, z + j, brick_z, length_x, 2 * brick_z) for j in range(2)], axis=1
        )
        out = dot3(gx, split(data))
        for j in range(2):
            part = out[:, j * lanes : (j + 1) * lanes]
            s4[pl.ds((z + j) * brick_x, brick_x), :lanes] = part[:brick_x]
            s4[pl.ds((z + j) * brick_x, brick_x), lanes:] = part[brick_x:]
    value = dot3(split(s4[...]), (iy_h[...], iy_l[...]))
    if conj:
        updated = own[...] * value
        cube = updated.reshape(brick_z, brick_x, brick_y)
        outs[0][...] = updated
        outs[1][...] = jnp.max(cube, axis=1)
        outs[2][...] = jnp.max(cube, axis=0)
        outs[3][...] = jnp.max(cube, axis=2)
    else:
        ratio = own[...] / value
        outs[0][...] = ratio
        outs[1][...] = packed_edges(ratio, groups)


def packed_edges(value, groups):
    rows, lanes = value.shape
    chunk = rows // groups
    width = lanes // groups
    lane = lax.broadcasted_iota(jnp.int32, (chunk, lanes), 1)
    out = pltpu.roll(value[:chunk], width // 2, 1)
    for g in range(1, groups):
        moved = pltpu.roll(value[g * chunk : (g + 1) * chunk], (width // 2 + g * width) % lanes, 1)
        out = jnp.where(lane >= g * width, moved, out)
    return out


def pack_body(value, out, *, groups):
    out[...] = packed_edges(value[...], groups)


def both_ways(value, axis):
    ends = lax.axis_size(axis) - 1
    ahead = lax.ppermute(value, axis, [(i, i + 1) for i in range(ends)])
    behind = lax.ppermute(value, axis, [(i + 1, i) for i in range(ends)])
    return ahead, behind


def surround(value, edges, margin):
    before, after = both_ways(edges, "gy")
    lane = lax.broadcasted_iota(jnp.int32, edges.shape, 1)
    halo = jnp.where(lane % (2 * margin) < margin, before, after)
    block = jnp.concatenate([value, halo], axis=0)
    low, high = both_ways(block, "gz")
    mid = jnp.concatenate([low, block, high], axis=0)
    left, right = both_ways(mid, "gx")
    return left, mid, right


def ring_max(value, axis):
    count = lax.axis_size(axis)
    if count <= 4:
        others = [
            lax.ppermute(value, axis, [(i, (i + s) % count) for i in range(count)]) for s in range(1, count)
        ]
        return functools.reduce(jnp.maximum, others, value)
    shift = 1
    while shift < count:
        moved = lax.ppermute(value, axis, [(i, (i + shift) % count) for i in range(count)])
        value = jnp.maximum(value, moved)
        shift *= 2
    return value


def shards(estimate, measured, point_spread):
    extent = point_spread.shape[0]
    margin = extent // 2
    brick = brick_z, brick_x, brick_y = estimate.shape
    assert brick_z == margin and brick_x == margin
    dims = length_z, length_x, length_y = tuple(n + extent for n in brick)
    lanes = -(-(length_y // 2 + 1) // 128) * 128
    groups = brick_y // extent
    rows = brick_z * brick_x
    chunk = rows // groups
    around_y = forward_right(length_y, np.arange(length_y), lanes)
    tables = np.zeros((groups, 2 * brick_y, 2 * lanes))
    for g in range(groups):
        tables[g, :brick_y] = around_y[margin : margin + brick_y]
        base = brick_y + g * extent
        tables[g, base : base + margin] = around_y[:margin]
        tables[g, base + margin : base + extent] = around_y[margin + brick_y :]
    inner = lambda n: np.arange(n) + margin
    conv_tables = (
        *constant(tables),
        *constant(forward_left(length_x, np.arange(length_x))),
        *constant(forward_left(length_z, np.arange(length_z))),
        *constant(inverse_left(length_z, inner(brick_z))),
        *constant(inverse_left(length_x, inner(brick_x))),
        *constant(inverse_right(length_y, inner(brick_y), lanes)),
    )
    offsets = np.arange(extent) - margin
    psf_tables = (
        *constant(forward_right(length_y, offsets, lanes)),
        *constant(forward_left(length_x, offsets)),
        *constant(forward_left(length_z, offsets)),
    )
    shape = jax.ShapeDtypeStruct
    scratch = lambda *s: pltpu.VMEM(s, F32)

    own = estimate.reshape(rows, brick_y)
    edges = pl.pallas_call(
        functools.partial(pack_body, groups=groups), out_shape=shape((chunk, brick_y), F32)
    )(own)
    spec = pl.pallas_call(
        functools.partial(spectrum_body, extent=extent, dims=dims, lanes=lanes),
        out_shape=shape((length_x * 2 * length_z, lanes), F32),
        scratch_shapes=[scratch(extent * extent, 2 * lanes), scratch(extent * 2 * length_x, lanes)],
    )(point_spread.reshape(extent * extent, extent), *psf_tables)

    def convolve(region, mate, conj, out_shape):
        return pl.pallas_call(
            functools.partial(conv_body, brick=brick, dims=dims, lanes=lanes, groups=groups, conj=conj),
            out_shape=out_shape,
            scratch_shapes=[
                scratch(length_z * length_x, 2 * lanes),
                scratch(length_z * 2 * length_x, lanes),
                scratch(length_x * 2 * brick_z, lanes),
                scratch(rows, 2 * lanes),
            ],
        )(*region, mate, spec, *conv_tables)

    ratio, ratio_edges = convolve(
        surround(own, edges, margin),
        measured.reshape(rows, brick_y),
        False,
        (shape((rows, brick_y), F32), shape((chunk, brick_y), F32)),
    )
    updated, across, top, along = convolve(
        surround(ratio, ratio_edges, margin),
        own,
        True,
        (
            shape((rows, brick_y), F32),
            shape((brick_z, brick_y), F32),
            shape((brick_x, brick_y), F32),
            shape((brick_z, brick_x), F32),
        ),
    )
    across = ring_max(across, "gx")
    along = ring_max(along, "gy")
    merged = ring_max(top, "gz")
    piece = brick_y // lax.axis_size("gz")
    top_view = lax.dynamic_slice_in_dim(merged, lax.axis_index("gz") * piece, piece, 1)
    return (updated.reshape(brick), across, along, top_view)


def solution(mesh):
    in_specs = (P("gz", "gx", "gy"), P("gz", "gx", "gy"), P())
    out_specs = (P("gz", "gx", "gy"), P("gz", "gy"), P("gz", "gx"), P("gx", ("gy", "gz")))
    return jax.shard_map(shards, mesh=mesh, in_specs=in_specs, out_specs=out_specs, check_vma=False)
```

profile of v0, /device:TPU:0, one launch (start us, length us, event | category | flops | bytes accessed | tf_op | source)
XLA Modules:
  0.0 114.9 jit_solution(6205961032371387463)
XLA Ops:
  0.6 1.6 %shard_map.228 = f32[64,128]{1,0:T(8,128)} custom-call(f32[256,128]{1,0:T(8,128)} %bitcast.3), custom_call_target="tpu_custom_call" | custom-call | tf_op jit(solution)/shard_map/pallas_call | solution.py:278
  2.3 4.9 %collective-permute-start = (f32[64,128]{1,0:T(8,128)}, f32[64,128]{1,0:T(8,128)S(1)}, u32[]{:S(2)}, u32[]{:S(2)}) collective-permute-start(f32[64,128]{1,0:T(8,128)} %shard_map.228), channel_id=1, source_target_pairs={{0,2},{2,4},{4,6},{1,3},{3,5},{5,7},{8,10},{10,12},{12,14},{9,11},... | collective-permute-start | bytes 98312 | tf_op jit(solution)/shard_map/ppermute | solution.py:211
  9.1 4.1 %collective-permute-done.1 = f32[64,128]{1,0:T(8,128)S(1)} collective-permute-done((f32[64,128]{1,0:T(8,128)}, f32[64,128]{1,0:T(8,128)S(1)}, u32[]{:S(2)}, u32[]{:S(2)}) %collective-permute-start.1) | collective-permute-done | bytes 32800 | tf_op jit(solution)/shard_map/ppermute | solution.py:212
  14.1 3.4 %collective-permute-start.2 = (f32[320,128]{1,0:T(8,128)S(1)}, f32[320,128]{1,0:T(8,128)S(1)}, u32[]{:S(2)}, u32[]{:S(2)}) collective-permute-start(f32[320,128]{1,0:T(8,128)S(1)} %pad_maximum_fusion.2), channel_id=1, source_target_pairs={{0,1},{2,3},{4,5},{6,7},{8,9},{10,11},{12,13},{14,15},{16,17},{18,... | collective-permute-start | bytes 491528 | tf_op jit(solution)/shard_map/ppermute | solution.py:211
  18.9 1.5 %collective-permute-done.2 = f32[320,128]{1,0:T(8,128)S(1)} collective-permute-done((f32[320,128]{1,0:T(8,128)S(1)}, f32[320,128]{1,0:T(8,128)S(1)}, u32[]{:S(2)}, u32[]{:S(2)}) %collective-permute-start.2) | collective-permute-done | bytes 163872 | tf_op jit(solution)/shard_map/ppermute | solution.py:211
  20.4 4.4 %collective-permute-done.3 = f32[320,128]{1,0:T(8,128)S(1)} collective-permute-done((f32[320,128]{1,0:T(8,128)S(1)}, f32[320,128]{1,0:T(8,128)S(1)}, u32[]{:S(2)}, u32[]{:S(2)}) %collective-permute-start.3) | collective-permute-done | bytes 163872 | tf_op jit(solution)/shard_map/ppermute | solution.py:212
  25.8 1.3 %collective-permute-start.4 = (f32[960,128]{1,0:T(8,128)S(1)}, f32[960,128]{1,0:T(8,128)S(1)}, u32[]{:S(2)}, u32[]{:S(2)}) collective-permute-start(f32[960,128]{1,0:T(8,128)S(1)} %pad_maximum_fusion.mid), channel_id=1, source_target_pairs={{0,8},{8,16},{16,24},{1,9},{9,17},{17,25},{2,10},{10,18},{18,26},{... | collective-permute-start | bytes 1474568 | tf_op jit(solution)/shard_map/ppermute | solution.py:211
  28.4 1.9 %reshape.22.psf = f32[1024,32]{1,0:T(8,128)} reshape(f32[32,1024]{1,0:T(8,128)} %param.23) | data formatting | bytes 262144 | tf_op jit(solution)/shard_map/reshape | solution.py:285
  30.3 6.5 %shard_map.229.spec = f32[4608,128]{1,0:T(8,128)} custom-call(f32[1024,32]{1,0:T(8,128)} %reshape.22.psf, bf16[32,256]{1,0:T(8,128)(2,1)} %constant.62.clone.ty_h, bf16[32,256]{1,0:T(8,128)(2,1)} %constant.63.clone.ty_l, bf16[96,64]{1,0:T(8,128)(2,1)} %constant.64.clone.fx_h.fz_h, bf16[96,64]{1,0:T(8,128)(2,1)} %constant.65.clone.fx_l.fz_l, ...), custom_call_target="tpu_custom_call" | custom-call | tf_op jit(solution)/shard_map/pallas_call | solution.py:281
  37.7 14.0 %shard_map.230 = (f32[256,128]{1,0:T(8,128)}, f32[64,128]{1,0:T(8,128)}) custom-call(f32[960,128]{1,0:T(8,128)} %copy-done.4, f32[960,128]{1,0:T(8,128)} %copy-done.1, f32[960,128]{1,0:T(8,128)} %copy-done.5, f32[256,128]{1,0:T(8,128)} %bitcast.7, f32[4608,128]{1,0:T(8,128)} %shard_map.229.spec, bf16[4,256,256]{2,1,0:T(8,128)(2,1)} %constant.54.clone.ty_h, ...), custom_call_target="tpu_custom_call" | custom-call | tf_op jit(solution)/shard_map/pallas_call | solution.py:288
  51.7 3.5 %collective-permute-start.6 = (f32[64,128]{1,0:T(8,128)}, f32[64,128]{1,0:T(8,128)S(1)}, u32[]{:S(2)}, u32[]{:S(2)}) collective-permute-start(f32[64,128]{1,0:T(8,128)} %get-tuple-element.11), channel_id=1, source_target_pairs={{0,2},{2,4},{4,6},{1,3},{3,5},{5,7},{8,10},{10,12},{12,14},{9,11},... | collective-permute-start | bytes 98312 | tf_op jit(solution)/shard_map/ppermute | solution.py:211
  57.0 4.1 %collective-permute-done.7 = f32[64,128]{1,0:T(8,128)S(1)} collective-permute-done((f32[64,128]{1,0:T(8,128)}, f32[64,128]{1,0:T(8,128)S(1)}, u32[]{:S(2)}, u32[]{:S(2)}) %collective-permute-start.7) | collective-permute-done | bytes 32800 | tf_op jit(solution)/shard_map/ppermute | solution.py:212
  62.1 1.5 %collective-permute-start.8 = (f32[320,128]{1,0:T(8,128)S(1)}, f32[320,128]{1,0:T(8,128)S(1)}, u32[]{:S(2)}, u32[]{:S(2)}) collective-permute-start(f32[320,128]{1,0:T(8,128)S(1)} %pad_maximum_fusion.3), channel_id=1, source_target_pairs={{0,1},{2,3},{4,5},{6,7},{8,9},{10,11},{12,13},{14,15},{16,17},{18,... | collective-permute-start | bytes 491528 | tf_op jit(solution)/shard_map/ppermute | solution.py:211
  64.9 2.7 %collective-permute-done.8 = f32[320,128]{1,0:T(8,128)S(1)} collective-permute-done((f32[320,128]{1,0:T(8,128)S(1)}, f32[320,128]{1,0:T(8,128)S(1)}, u32[]{:S(2)}, u32[]{:S(2)}) %collective-permute-start.8) | collective-permute-done | bytes 163872 | tf_op jit(solution)/shard_map/ppermute | solution.py:211
  67.6 4.7 %collective-permute-done.9 = f32[320,128]{1,0:T(8,128)S(1)} collective-permute-done((f32[320,128]{1,0:T(8,128)S(1)}, f32[320,128]{1,0:T(8,128)S(1)}, u32[]{:S(2)}, u32[]{:S(2)}) %collective-permute-start.9) | collective-permute-done | bytes 163872 | tf_op jit(solution)/shard_map/ppermute | solution.py:212
  73.2 2.0 %collective-permute-start.10 = (f32[960,128]{1,0:T(8,128)S(1)}, f32[960,128]{1,0:T(8,128)S(1)}, u32[]{:S(2)}, u32[]{:S(2)}) collective-permute-start(f32[960,128]{1,0:T(8,128)S(1)} %pad_maximum_fusion.1.mid), channel_id=1, source_target_pairs={{0,8},{8,16},{16,24},{1,9},{9,17},{17,25},{2,10},{10,18},{18,26},{... | collective-permute-start | bytes 1474568 | tf_op jit(solution)/shard_map/ppermute | solution.py:211
  76.7 4.8 %collective-permute-done.11.right = f32[960,128]{1,0:T(8,128)S(1)} collective-permute-done((f32[960,128]{1,0:T(8,128)S(1)}, f32[960,128]{1,0:T(8,128)S(1)}, u32[]{:S(2)}, u32[]{:S(2)}) %collective-permute-start.11) | collective-permute-done | bytes 491552 | tf_op jit(solution)/shard_map/ppermute | solution.py:212
  82.3 14.0 %shard_map.231 = (f32[256,128]{1,0:T(8,128)}, f32[16,128]{1,0:T(8,128)}, f32[16,128]{1,0:T(8,128)}, f32[16,16]{1,0:T(8,128)}) custom-call(f32[960,128]{1,0:T(8,128)} %copy-done.2, f32[960,128]{1,0:T(8,128)} %copy-done, f32[960,128]{1,0:T(8,128)} %copy-done.3, f32[256,128]{1,0:T(8,128)} %bitcast.6, f32[4608,128]{1,0:T(8,128)} %shard_map.229.spec, ...), custom_call_target="tpu_custom_call" | custom-call | tf_op jit(solution)/shard_map/pallas_call | solution.py:288
  96.2 1.6 %collective-permute-start.15 = (f32[16,16]{1,0:T(8,128)}, f32[16,16]{1,0:T(8,128)S(1)}, u32[]{:S(2)}, u32[]{:S(2)}) collective-permute-start(f32[16,16]{1,0:T(8,128)} %get-tuple-element.14), channel_id=1, source_target_pairs={{0,2},{2,4},{4,6},{6,0},{1,3},{3,5},{5,7},{7,1},{8,10},{10,12},{12... | collective-permute-start | bytes 3080 | tf_op jit(solution)/shard_map/ppermute | solution.py:231
  97.8 2.4 %collective-permute-start.17 = (f32[16,16]{1,0:T(8,128)}, f32[16,16]{1,0:T(8,128)S(1)}, u32[]{:S(2)}, u32[]{:S(2)}) collective-permute-start(f32[16,16]{1,0:T(8,128)} %get-tuple-element.14), channel_id=1, source_target_pairs={{0,6},{2,0},{4,2},{6,4},{1,7},{3,1},{5,3},{7,5},{8,14},{10,8},{12,... | collective-permute-start | bytes 3080 | tf_op jit(solution)/shard_map/ppermute | solution.py:231
  100.2 6.3 %collective-permute-start.12 = (f32[16,128]{1,0:T(8,128)}, f32[16,128]{1,0:T(8,128)S(1)}, u32[]{:S(2)}, u32[]{:S(2)}) collective-permute-start(f32[16,128]{1,0:T(8,128)} %get-tuple-element.13), channel_id=1, source_target_pairs={{0,8},{8,16},{16,24},{24,0},{1,9},{9,17},{17,25},{25,1},{2,10},{10... | collective-permute-start | bytes 24584 | tf_op jit(solution)/shard_map/ppermute | solution.py:231
  106.9 1.5 %collective-permute-start.14 = (f32[16,128]{1,0:T(8,128)}, f32[16,128]{1,0:T(8,128)S(1)}, u32[]{:S(2)}, u32[]{:S(2)}) collective-permute-start(f32[16,128]{1,0:T(8,128)} %get-tuple-element.13), channel_id=1, source_target_pairs={{0,24},{8,0},{16,8},{24,16},{1,25},{9,1},{17,9},{25,17},{2,26},{10... | collective-permute-start | bytes 24584 | tf_op jit(solution)/shard_map/ppermute | solution.py:231
  109.6 2.6 %collective-permute-done.18 = f32[16,128]{1,0:T(8,128)S(1)} collective-permute-done((f32[16,128]{1,0:T(8,128)}, f32[16,128]{1,0:T(8,128)S(1)}, u32[]{:S(2)}, u32[]{:S(2)}) %collective-permute-start.18) | collective-permute-done | bytes 8224 | tf_op jit(solution)/shard_map/ppermute | solution.py:231
  112.2 1.4 %dynamic-slice_maximum_fusion = f32[16,64]{1,0:T(8,128)} fusion(f32[16,128]{1,0:T(8,128)S(1)} %collective-permute-done.18, s32[]{:T(128)S(6)} %select_n.24, f32[16,128]{1,0:T(8,128)} %get-tuple-element.15), kind=kLoop, calls=%fused_computation.7 | loop fusion | flops 1024 | bytes 12292 | tf_op jit(solution)/shard_map/max | solution.py:233
  (43 shorter events, 17.4 us)
Async XLA Ops:
  2.3 6.8 %collective-permute-start = (f32[64,128]{1,0:T(8,128)}, f32[64,128]{1,0:T(8,128)S(1)}, u32[]{:S(2)}, u32[]{:S(2)}) collective-permute-start(f32[64,128]{1,0:T(8,128)} %shard_map.228), channel_id=1, source_target_pairs={{0,2},{2,4},{4,6},{1,3},{3,5},{5,7},{8,10},{10,12},{12,14},{9,11},... | collective-permute-start | bytes 98312 | tf_op jit(solution)/shard_map/ppermute | solution.py:211
  7.2 6.0 %collective-permute-start.1 = (f32[64,128]{1,0:T(8,128)}, f32[64,128]{1,0:T(8,128)S(1)}, u32[]{:S(2)}, u32[]{:S(2)}) collective-permute-start(f32[64,128]{1,0:T(8,128)} %shard_map.228), channel_id=1, source_target_pairs={{2,0},{4,2},{6,4},{3,1},{5,3},{7,5},{10,8},{12,10},{14,12},{11,9},... | collective-permute-start | bytes 98312 | tf_op jit(solution)/shard_map/ppermute | solution.py:212
  14.1 6.3 %collective-permute-start.2 = (f32[320,128]{1,0:T(8,128)S(1)}, f32[320,128]{1,0:T(8,128)S(1)}, u32[]{:S(2)}, u32[]{:S(2)}) collective-permute-start(f32[320,128]{1,0:T(8,128)S(1)} %pad_maximum_fusion.2), channel_id=1, source_target_pairs={{0,1},{2,3},{4,5},{6,7},{8,9},{10,11},{12,13},{14,15},{16,17},{18,... | collective-permute-start | bytes 491528 | tf_op jit(solution)/shard_map/ppermute | solution.py:211
  17.6 7.2 %collective-permute-start.3 = (f32[320,128]{1,0:T(8,128)S(1)}, f32[320,128]{1,0:T(8,128)S(1)}, u32[]{:S(2)}, u32[]{:S(2)}) collective-permute-start(f32[320,128]{1,0:T(8,128)S(1)} %pad_maximum_fusion.2), channel_id=1, source_target_pairs={{1,0},{3,2},{5,4},{7,6},{9,8},{11,10},{13,12},{15,14},{17,16},{19,... | collective-permute-start | bytes 491528 | tf_op jit(solution)/shard_map/ppermute | solution.py:212
  25.7 11.1 %copy-start.1 = (f32[960,128]{1,0:T(8,128)}, f32[960,128]{1,0:T(8,128)S(1)}, u32[]{:S(2)}) copy-start(f32[960,128]{1,0:T(8,128)S(1)} %pad_maximum_fusion.mid) | copy-start | bytes 1474564
  25.8 11.0 %collective-permute-start.4 = (f32[960,128]{1,0:T(8,128)S(1)}, f32[960,128]{1,0:T(8,128)S(1)}, u32[]{:S(2)}, u32[]{:S(2)}) collective-permute-start(f32[960,128]{1,0:T(8,128)S(1)} %pad_maximum_fusion.mid), channel_id=1, source_target_pairs={{0,8},{8,16},{16,24},{1,9},{9,17},{17,25},{2,10},{10,18},{18,26},{... | collective-permute-start | bytes 1474568 | tf_op jit(solution)/shard_map/ppermute | solution.py:211
  27.1 9.7 %collective-permute-start.5 = (f32[960,128]{1,0:T(8,128)S(1)}, f32[960,128]{1,0:T(8,128)S(1)}, u32[]{:S(2)}, u32[]{:S(2)}) collective-permute-start(f32[960,128]{1,0:T(8,128)S(1)} %pad_maximum_fusion.mid), channel_id=1, source_target_pairs={{8,0},{16,8},{24,16},{9,1},{17,9},{25,17},{10,2},{18,10},{26,18},{... | collective-permute-start | bytes 1474568 | tf_op jit(solution)/shard_map/ppermute | solution.py:212
  36.8 0.8 copy-start.4
  36.8 0.9 copy-start.5
  51.7 5.4 %collective-permute-start.6 = (f32[64,128]{1,0:T(8,128)}, f32[64,128]{1,0:T(8,128)S(1)}, u32[]{:S(2)}, u32[]{:S(2)}) collective-permute-start(f32[64,128]{1,0:T(8,128)} %get-tuple-element.11), channel_id=1, source_target_pairs={{0,2},{2,4},{4,6},{1,3},{3,5},{5,7},{8,10},{10,12},{12,14},{9,11},... | collective-permute-start | bytes 98312 | tf_op jit(solution)/shard_map/ppermute | solution.py:211
  55.2 6.0 %collective-permute-start.7 = (f32[64,128]{1,0:T(8,128)}, f32[64,128]{1,0:T(8,128)S(1)}, u32[]{:S(2)}, u32[]{:S(2)}) collective-permute-start(f32[64,128]{1,0:T(8,128)} %get-tuple-element.11), channel_id=1, source_target_pairs={{2,0},{4,2},{6,4},{3,1},{5,3},{7,5},{10,8},{12,10},{14,12},{11,9},... | collective-permute-start | bytes 98312 | tf_op jit(solution)/shard_map/ppermute | solution.py:212
  62.1 5.5 %collective-permute-start.8 = (f32[320,128]{1,0:T(8,128)S(1)}, f32[320,128]{1,0:T(8,128)S(1)}, u32[]{:S(2)}, u32[]{:S(2)}) collective-permute-start(f32[320,128]{1,0:T(8,128)S(1)} %pad_maximum_fusion.3), channel_id=1, source_target_pairs={{0,1},{2,3},{4,5},{6,7},{8,9},{10,11},{12,13},{14,15},{16,17},{18,... | collective-permute-start | bytes 491528 | tf_op jit(solution)/shard_map/ppermute | solution.py:211
  63.6 8.7 %collective-permute-start.9 = (f32[320,128]{1,0:T(8,128)S(1)}, f32[320,128]{1,0:T(8,128)S(1)}, u32[]{:S(2)}, u32[]{:S(2)}) collective-permute-start(f32[320,128]{1,0:T(8,128)S(1)} %pad_maximum_fusion.3), channel_id=1, source_target_pairs={{1,0},{3,2},{5,4},{7,6},{9,8},{11,10},{13,12},{15,14},{17,16},{19,... | collective-permute-start | bytes 491528 | tf_op jit(solution)/shard_map/ppermute | solution.py:212
  73.2 8.3 %copy-start = (f32[960,128]{1,0:T(8,128)}, f32[960,128]{1,0:T(8,128)S(1)}, u32[]{:S(2)}) copy-start(f32[960,128]{1,0:T(8,128)S(1)} %pad_maximum_fusion.1.mid) | copy-start | bytes 1474564
  73.2 3.5 %collective-permute-start.10 = (f32[960,128]{1,0:T(8,128)S(1)}, f32[960,128]{1,0:T(8,128)S(1)}, u32[]{:S(2)}, u32[]{:S(2)}) collective-permute-start(f32[960,128]{1,0:T(8,128)S(1)} %pad_maximum_fusion.1.mid), channel_id=1, source_target_pairs={{0,8},{8,16},{16,24},{1,9},{9,17},{17,25},{2,10},{10,18},{18,26},{... | collective-permute-start | bytes 1474568 | tf_op jit(solution)/shard_map/ppermute | solution.py:211
  75.3 6.2 %collective-permute-start.11 = (f32[960,128]{1,0:T(8,128)S(1)}, f32[960,128]{1,0:T(8,128)S(1)}, u32[]{:S(2)}, u32[]{:S(2)}) collective-permute-start(f32[960,128]{1,0:T(8,128)S(1)} %pad_maximum_fusion.1.mid), channel_id=1, source_target_pairs={{8,0},{16,8},{24,16},{9,1},{17,9},{25,17},{10,2},{18,10},{26,18},{... | collective-permute-start | bytes 1474568 | tf_op jit(solution)/shard_map/ppermute | solution.py:212
  76.7 4.8 %copy-start.2 = (f32[960,128]{1,0:T(8,128)}, f32[960,128]{1,0:T(8,128)S(1)}, u32[]{:S(2)}) copy-start(f32[960,128]{1,0:T(8,128)S(1)} %collective-permute-done.10.left) | copy-start | bytes 1474564
  96.2 10.7 %collective-permute-start.15 = (f32[16,16]{1,0:T(8,128)}, f32[16,16]{1,0:T(8,128)S(1)}, u32[]{:S(2)}, u32[]{:S(2)}) collective-permute-start(f32[16,16]{1,0:T(8,128)} %get-tuple-element.14), channel_id=1, source_target_pairs={{0,2},{2,4},{4,6},{6,0},{1,3},{3,5},{5,7},{7,1},{8,10},{10,12},{12... | collective-permute-start | bytes 3080 | tf_op jit(solution)/shard_map/ppermute | solution.py:231
  97.8 10.5 %collective-permute-start.16 = (f32[16,16]{1,0:T(8,128)}, f32[16,16]{1,0:T(8,128)S(1)}, u32[]{:S(2)}, u32[]{:S(2)}) collective-permute-start(f32[16,16]{1,0:T(8,128)} %get-tuple-element.14), channel_id=1, source_target_pairs={{0,4},{2,6},{4,0},{6,2},{1,5},{3,7},{5,1},{7,3},{8,12},{10,14},{12... | collective-permute-start | bytes 3080 | tf_op jit(solution)/shard_map/ppermute | solution.py:231
  97.8 10.5 %collective-permute-start.17 = (f32[16,16]{1,0:T(8,128)}, f32[16,16]{1,0:T(8,128)S(1)}, u32[]{:S(2)}, u32[]{:S(2)}) collective-permute-start(f32[16,16]{1,0:T(8,128)} %get-tuple-element.14), channel_id=1, source_target_pairs={{0,6},{2,0},{4,2},{6,4},{1,7},{3,1},{5,3},{7,5},{8,14},{10,8},{12,... | collective-permute-start | bytes 3080 | tf_op jit(solution)/shard_map/ppermute | solution.py:231
  100.2 13.3 %collective-permute-start.12 = (f32[16,128]{1,0:T(8,128)}, f32[16,128]{1,0:T(8,128)S(1)}, u32[]{:S(2)}, u32[]{:S(2)}) collective-permute-start(f32[16,128]{1,0:T(8,128)} %get-tuple-element.13), channel_id=1, source_target_pairs={{0,8},{8,16},{16,24},{24,0},{1,9},{9,17},{17,25},{25,1},{2,10},{10... | collective-permute-start | bytes 24584 | tf_op jit(solution)/shard_map/ppermute | solution.py:231
  106.6 7.0 %collective-permute-start.13 = (f32[16,128]{1,0:T(8,128)}, f32[16,128]{1,0:T(8,128)S(1)}, u32[]{:S(2)}, u32[]{:S(2)}) collective-permute-start(f32[16,128]{1,0:T(8,128)} %get-tuple-element.13), channel_id=1, source_target_pairs={{0,16},{8,24},{16,0},{24,8},{1,17},{9,25},{17,1},{25,9},{2,18},{10... | collective-permute-start | bytes 24584 | tf_op jit(solution)/shard_map/ppermute | solution.py:231
  106.9 6.7 %collective-permute-start.14 = (f32[16,128]{1,0:T(8,128)}, f32[16,128]{1,0:T(8,128)S(1)}, u32[]{:S(2)}, u32[]{:S(2)}) collective-permute-start(f32[16,128]{1,0:T(8,128)} %get-tuple-element.13), channel_id=1, source_target_pairs={{0,24},{8,0},{16,8},{24,16},{1,25},{9,1},{17,9},{25,17},{2,26},{10... | collective-permute-start | bytes 24584 | tf_op jit(solution)/shard_map/ppermute | solution.py:231
  108.3 3.9 %collective-permute-start.18 = (f32[16,128]{1,0:T(8,128)}, f32[16,128]{1,0:T(8,128)S(1)}, u32[]{:S(2)}, u32[]{:S(2)}) collective-permute-start(f32[16,128]{1,0:T(8,128)} %get-tuple-element.15), channel_id=1, source_target_pairs={{0,1},{1,0},{2,3},{3,2},{4,5},{5,4},{6,7},{7,6},{8,9},{9,8},{10,11... | collective-permute-start | bytes 24584 | tf_op jit(solution)/shard_map/ppermute | solution.py:231
  (1 other events, 0.8 us)
where the time goes:
time: 116 us; the launch traced here: 115 us
  starting transfers between devices  36.5 us (31%)
  Pallas kernels  36.1 us (31%)
  waiting for transfers between devices  30.2 us (26%)
  other arithmetic  7.7 us (7%)
  local copies, waits for them, and re-layouts  3.59 us (3%)
    pallas_call x2, Pallas kernels, convolve(): pl.pallas_call(functools.partial(conv_body, brick=brick, dims=dims, lanes...  27.9 us
    ppermute x6, waiting for transfers between devices, both_ways(): behind = lax.ppermute(value, axis, [(i + 1, i) for i in range(ends)])  22.1 us
    ppermute x6, starting transfers between devices, both_ways(): ahead = lax.ppermute(value, axis, [(i, i + 1) for i in range(ends)])  16.7 us
    ppermute x7, starting transfers between devices, ring_max(): lax.ppermute(value, axis, [(i, (i + s) % count) for i in range(count)])  12.1 us
    ppermute x6, starting transfers between devices, both_ways(): behind = lax.ppermute(value, axis, [(i + 1, i) for i in range(ends)])  7.75 us
    pallas_call x1, Pallas kernels, shards(): pl.pallas_call(functools.partial(spectrum_body, extent=extent, dims=dims,...  6.53 us
    ppermute x6, waiting for transfers between devices, both_ways(): ahead = lax.ppermute(value, axis, [(i, i + 1) for i in range(ends)])  5.51 us
    max x3, other arithmetic, ring_max(): return functools.reduce(jnp.maximum, others, value)  3.97 us
  transfers between devices with their start and end apart: 19, of which 11 were waited for; matrix products, arithmetic and copies ran while one was open for 4% of the time, Pallas kernels for 6%

commit v1 on v0

--- a/solution.py
+++ b/solution.py
@@ -21,12 +21,29 @@
     table = np.asarray(table, np.float32)
     high = table.astype(BF16)
     low = (table - high.astype(np.float32)).astype(BF16)
-    return jnp.asarray(high), jnp.asarray(low)
-
-
-def dot3(left, right):
-    mul = functools.partial(jnp.dot, preferred_element_type=F32)
-    return mul(left[0], right[0]) + (mul(left[0], right[1]) + mul(left[1], right[0]))
+    return high, low
+
+
+def stacked(table):
+    return jnp.asarray(np.concatenate(constant(table), axis=-2))
+
+
+def mul(left, right):
+    return jnp.dot(left, right, preferred_element_type=F32)
+
+
+def table_dot(table, data):
+    high, low = split(data)
+    half = table.shape[0] // 2
+    out = mul(table, high)
+    return out[:half] + (out[half:] + mul(table[:half], low))
+
+
+def dot_table(data, table_high, table_low):
+    both = jnp.concatenate(split(data), axis=0)
+    half = data.shape[0]
+    out = mul(both, table_high)
+    return out[:half] + (out[half:] + mul(both[:half], table_low))
 
 
 def angles(rows, cols, length):
@@ -82,7 +99,7 @@
         data = jnp.concatenate(
             [pair_x(s1, (z + j) * count_x, count_x, lanes) for j in range(2)], axis=1
         )
-        out = dot3(table, split(data))
+        out = table_dot(table, data)
         for j in range(2):
             s2[pl.ds((z + j) * 2 * length_x, 2 * length_x), :] = out[:, j * lanes : (j + 1) * lanes]
         return carry
@@ -90,20 +107,20 @@
     lax.fori_loop(0, count_z // 2, step, 0, unroll=4)
 
 
-def spectrum_body(psf, ty_h, ty_l, fx_h, fx_l, fz_h, fz_l, spec, s1, s2, *, extent, dims, lanes):
+def spectrum_body(psf, ty_h, ty_l, fx, fz, spec, s1, s2, *, extent, dims, lanes):
     length_z, length_x, length_y = dims
     values = psf[...]
     scale = 1.0 / (jnp.sum(values) * float(length_z * length_x * length_y))
-    s1[...] = dot3(split(values), (ty_h[...], ty_l[...])) * scale
-    transform_x(s1, s2, (fx_h[...], fx_l[...]), extent, extent, length_x, lanes)
-    table = (fz_h[...], fz_l[...])
+    s1[...] = dot_table(values, ty_h[...], ty_l[...]) * scale
+    transform_x(s1, s2, fx[...], extent, extent, length_x, lanes)
+    table = fz[...]
 
     def step(i, carry):
         k = i * 2
         data = jnp.concatenate(
             [pair_strided(s2, k + j, length_x, extent, 2 * length_x) for j in range(2)], axis=1
         )
-        out = dot3(table, split(data))
+        out = table_dot(table, data)
         for j in range(2):
             spec[pl.ds((k + j) * 2 * length_z, 2 * length_z), :] = out[:, j * lanes : (j + 1) * lanes]
         return carry
@@ -111,46 +128,43 @@
     lax.fori_loop(0, length_x // 2, step, 0, unroll=4)
 
 
-def conv_body(
-    left, mid, right, own, spec, ty_h, ty_l, fx_h, fx_l, fz_h, fz_l, gz_h, gz_l, gx_h, gx_l, iy_h, iy_l,
-    *rest, brick, dims, lanes, groups, conj,
-):
-    outs, (s1, s2, s3, s4) = rest[:-4], rest[-4:]
+def conv_body(place, *refs, brick, dims, lanes, groups, parts, conj):
+    parts_z, parts_x = parts
+    count = parts_z * parts_x
+    region, refs = refs[:count], refs[count:]
+    own, spec, ty_h, ty_l, fx, fz, gz, gx, iy_h, iy_l = refs[:10]
+    outs, (s1, s2, s3, s4) = refs[10:-4], refs[-4:]
     brick_z, brick_x, brick_y = brick
     length_z, length_x, length_y = dims
     rows = brick_z * brick_x
     chunk = rows // groups
-    block = rows + chunk
+    per = chunk // brick_x
+    wide_z, wide_x = parts_z * brick_z, parts_x * brick_x
     for g in range(groups):
-        table = (ty_h[g], ty_l[g])
-        for bx, ref in enumerate((left, mid, right)):
-            data = jnp.concatenate(
-                [
-                    jnp.concatenate(
-                        [ref[pl.ds(b * block + g * chunk, chunk), :], ref[pl.ds(b * block + rows, chunk), :]],
-                        axis=1,
-                    )
-                    for b in range(3)
-                ],
-                axis=0,
-            )
-            out = dot3(split(data), table)
-            per = chunk // brick_x
-            for b in range(3):
-                for zi in range(per):
-                    z = b * brick_z + g * per + zi
-                    src = b * chunk + zi * brick_x
-                    s1[pl.ds(z * length_x + bx * brick_x, brick_x), :] = out[src : src + brick_x]
-    transform_x(s1, s2, (fx_h[...], fx_l[...]), length_z, length_x, length_x, lanes)
-    fz = (fz_h[...], fz_l[...])
-    gz = (gz_h[...], gz_l[...])
+        data = jnp.concatenate(
+            [
+                jnp.concatenate([ref[pl.ds(g * chunk, chunk), :], ref[pl.ds(rows, chunk), :]], axis=1)
+                for ref in region
+            ],
+            axis=0,
+        )
+        out = dot_table(data, ty_h[g], ty_l[g])
+        for n in range(count):
+            bz, bx = n // parts_x, n % parts_x
+            for zi in range(per):
+                z = bz * brick_z + g * per + zi
+                src = n * chunk + zi * brick_x
+                s1[pl.ds(z * wide_x + bx * brick_x, brick_x), :] = out[src : src + brick_x]
+    transform_x(s1, s2, fx[place[0]], wide_z, wide_x, length_x, lanes)
+    forward_z = fz[place[1]]
+    back_z = gz[...]
 
     def middle(i, carry):
         k = i * 2
         data = jnp.concatenate(
-            [pair_strided(s2, k + j, length_x, length_z, 2 * length_x) for j in range(2)], axis=1
-        )
-        out = dot3(fz, split(data))
+            [pair_strided(s2, k + j, length_x, wide_z, 2 * length_x) for j in range(2)], axis=1
+        )
+        out = table_dot(forward_z, data)
         kern = jnp.concatenate(
             [spec[pl.ds((k + j) * 2 * length_z, 2 * length_z), :] for j in range(2)], axis=1
         )
@@ -160,23 +174,23 @@
             prod = jnp.concatenate([re * kr + im * ki, im * kr - re * ki], axis=0)
         else:
             prod = jnp.concatenate([re * kr - im * ki, re * ki + im * kr], axis=0)
-        back = dot3(gz, split(prod))
+        back = table_dot(back_z, prod)
         for j in range(2):
             s3[pl.ds((k + j) * 2 * brick_z, 2 * brick_z), :] = back[:, j * lanes : (j + 1) * lanes]
         return carry
 
     lax.fori_loop(0, length_x // 2, middle, 0, unroll=4)
-    gx = (gx_h[...], gx_l[...])
+    back_x = gx[...]
     for z in range(0, brick_z, 2):
         data = jnp.concatenate(
             [pair_strided(s3, z + j, brick_z, length_x, 2 * brick_z) for j in range(2)], axis=1
         )
-        out = dot3(gx, split(data))
+        out = table_dot(back_x, data)
         for j in range(2):
             part = out[:, j * lanes : (j + 1) * lanes]
             s4[pl.ds((z + j) * brick_x, brick_x), :lanes] = part[:brick_x]
             s4[pl.ds((z + j) * brick_x, brick_x), lanes:] = part[brick_x:]
-    value = dot3(split(s4[...]), (iy_h[...], iy_l[...]))
+    value = dot_table(s4[...], iy_h[...], iy_l[...])
     if conj:
         updated = own[...] * value
         cube = updated.reshape(brick_z, brick_x, brick_y)
@@ -206,37 +220,52 @@
     out[...] = packed_edges(value[...], groups)
 
 
-def both_ways(value, axis):
-    ends = lax.axis_size(axis) - 1
-    ahead = lax.ppermute(value, axis, [(i, i + 1) for i in range(ends)])
-    behind = lax.ppermute(value, axis, [(i + 1, i) for i in range(ends)])
-    return ahead, behind
+def swaps(value, axis):
+    count = lax.axis_size(axis)
+    found = []
+    for first in range(min(2, count - 1)):
+        pairs = [(i, i + 1) for i in range(first, count - 1, 2)]
+        found.append(lax.ppermute(value, axis, pairs + [(j, i) for i, j in pairs]))
+    return found
 
 
 def surround(value, edges, margin):
-    before, after = both_ways(edges, "gy")
+    sides = swaps(edges, "gy") + [jnp.zeros_like(edges)] * 2
     lane = lax.broadcasted_iota(jnp.int32, edges.shape, 1)
-    halo = jnp.where(lane % (2 * margin) < margin, before, after)
+    odd = lax.axis_index("gy") % 2 == 1
+    halo = jnp.where((lane % (2 * margin) < margin) == odd, sides[0], sides[1])
     block = jnp.concatenate([value, halo], axis=0)
-    low, high = both_ways(block, "gz")
-    mid = jnp.concatenate([low, block, high], axis=0)
-    left, right = both_ways(mid, "gx")
-    return left, mid, right
-
-
-def ring_max(value, axis):
-    count = lax.axis_size(axis)
-    if count <= 4:
-        others = [
-            lax.ppermute(value, axis, [(i, (i + s) % count) for i in range(count)]) for s in range(1, count)
-        ]
-        return functools.reduce(jnp.maximum, others, value)
+    above = swaps(block, "gz")
+    around = swaps(block, "gx")
+    region = [block, *around]
+    for part in above:
+        region += [part, *swaps(part, "gx")]
+    return region
+
+
+def spots(count, brick, margin):
+    own, low, high = np.arange(brick) + margin, np.arange(margin), np.arange(margin) + margin + brick
+    kept = min(3, count)
+    return [np.concatenate([own, high, low][:kept]), np.concatenate([own, low, high][:kept])]
+
+
+def all_max(items):
+    items = list(items)
     shift = 1
-    while shift < count:
-        moved = lax.ppermute(value, axis, [(i, (i + shift) % count) for i in range(count)])
-        value = jnp.maximum(value, moved)
+    while any(shift < lax.axis_size(axis) for _, axis in items):
+        moved = []
+        for value, axis in items:
+            count = lax.axis_size(axis)
+            if shift < count:
+                pairs = [(i, (i + shift) % count) for i in range(count)]
+                if count & (count - 1) == 0:
+                    pairs = [(i, i ^ shift) for i in range(count)]
+                moved.append(lax.ppermute(value, axis, pairs))
+            else:
+                moved.append(value)
+        items = [(jnp.maximum(value, new), axis) for (value, axis), new in zip(items, moved)]
         shift *= 2
-    return value
+    return [value for value, _ in items]
 
 
 def shards(estimate, measured, point_spread):
@@ -257,20 +286,24 @@
         tables[g, base : base + margin] = around_y[:margin]
         tables[g, base + margin : base + extent] = around_y[margin + brick_y :]
     inner = lambda n: np.arange(n) + margin
+    parts = parts_z, parts_x = tuple(min(3, lax.axis_size(axis)) for axis in ("gz", "gx"))
+    spots_x = spots(lax.axis_size("gx"), brick_x, margin)
+    spots_z = spots(lax.axis_size("gz"), brick_z, margin)
     conv_tables = (
-        *constant(tables),
-        *constant(forward_left(length_x, np.arange(length_x))),
-        *constant(forward_left(length_z, np.arange(length_z))),
-        *constant(inverse_left(length_z, inner(brick_z))),
-        *constant(inverse_left(length_x, inner(brick_x))),
-        *constant(inverse_right(length_y, inner(brick_y), lanes)),
+        *map(jnp.asarray, constant(tables)),
+        stacked(np.stack([forward_left(length_x, spot) for spot in spots_x])),
+        stacked(np.stack([forward_left(length_z, spot) for spot in spots_z])),
+        stacked(inverse_left(length_z, inner(brick_z))),
+        stacked(inverse_left(length_x, inner(brick_x))),
+        *map(jnp.asarray, constant(inverse_right(length_y, inner(brick_y), lanes))),
     )
     offsets = np.arange(extent) - margin
     psf_tables = (
-        *constant(forward_right(length_y, offsets, lanes)),
-        *constant(forward_left(length_x, offsets)),
-        *constant(forward_left(length_z, offsets)),
-    )
+        *map(jnp.asarray, constant(forward_right(length_y, offsets, lanes))),
+        stacked(forward_left(length_x, offsets)),
+        stacked(forward_left(length_z, offsets)),
+    )
+    place = jnp.stack([lax.axis_index("gx") % 2, lax.axis_index("gz") % 2]).astype(jnp.int32)
     shape = jax.ShapeDtypeStruct
     scratch = lambda *s: pltpu.VMEM(s, F32)
 
@@ -286,15 +319,17 @@
 
     def convolve(region, mate, conj, out_shape):
         return pl.pallas_call(
-            functools.partial(conv_body, brick=brick, dims=dims, lanes=lanes, groups=groups, conj=conj),
+            functools.partial(conv_body, brick=brick, dims=dims, lanes=lanes, groups=groups, parts=parts, conj=conj),
             out_shape=out_shape,
+            in_specs=[pl.BlockSpec(memory_space=pltpu.SMEM)]
+            + [pl.BlockSpec(memory_space=pltpu.VMEM)] * (len(region) + 2 + len(conv_tables)),
             scratch_shapes=[
-                scratch(length_z * length_x, 2 * lanes),
-                scratch(length_z * 2 * length_x, lanes),
+                scratch(parts_z * brick_z * parts_x * brick_x, 2 * lanes),
+                scratch(parts_z * brick_z * 2 * length_x, lanes),
                 scratch(length_x * 2 * brick_z, lanes),
                 scratch(rows, 2 * lanes),
             ],
-        )(*region, mate, spec, *conv_tables)
+        )(place, *region, mate, spec, *conv_tables)
 
     ratio, ratio_edges = convolve(
         surround(own, edges, margin),
@@ -313,9 +348,7 @@
             shape((brick_z, brick_x), F32),
         ),
     )
-    across = ring_max(across, "gx")
-    along = ring_max(along, "gy")
-    merged = ring_max(top, "gz")
+    merged, across, along = all_max([(top, "gz"), (across, "gx"), (along, "gy")])
     piece = brick_y // lax.axis_size("gz")
     top_view = lax.dynamic_slice_in_dim(merged, lax.axis_index("gz") * piece, piece, 1)
     return (updated.reshape(brick), across, along, top_view)

time: 116 us -> 91.3 us (0.79)
  waiting for transfers between devices: 30.2 us -> 11.3 us
  Pallas kernels: 36.1 us -> 32.7 us
  other arithmetic: 7.7 us -> 6.49 us
    ppermute x19, waiting for transfers between devices: 30.2 us -> 11.3 us  [the longest x14 7.2 us: swaps(): found.append(lax.ppermute(value, axis, pairs + [(j, i) for i, j in pairs]))]
    pallas_call x2, Pallas kernels: 27.9 us -> 24.6 us  [convolve(): pl.pallas_call(functools.partial(conv_body, brick=brick, dims=dims, lanes...]
    concatenate x2 -> x0, other arithmetic: 1.87 us -> none  [surround(): mid = jnp.concatenate([low, block, high], axis=0)]
    max x3 -> x5, other arithmetic: 3.97 us -> 3.97 us  [all_max(): jnp.maximum(value, new)]
  transfers between devices with their start and end apart: 19 -> 19, of which waited for: 11 -> 8; matrix products, arithmetic and copies ran while one was open for 4% -> 7% of each run, Pallas kernels for 6% -> 7%
where the time goes in v1:
time: 91.3 us; the launch traced here: 90.8 us
  starting transfers between devices  36.2 us (40%)
  Pallas kernels  32.7 us (36%)
  waiting for transfers between devices  11.3 us (12%)
  other arithmetic  6.49 us (7%)
  local copies, waits for them, and re-layouts  3.36 us (4%)
    ppermute x14, starting transfers between devices, swaps(): found.append(lax.ppermute(value, axis, pairs + [(j, i) for i, j in pairs]))  25.4 us
    pallas_call x2, Pallas kernels, convolve(): pl.pallas_call(functools.partial(conv_body, brick=brick, dims=dims, lanes...  24.6 us
    ppermute x5, starting transfers between devices, all_max(): moved.append(lax.ppermute(value, axis, pairs))  10.7 us
    ppermute x14, waiting for transfers between devices, swaps(): found.append(lax.ppermute(value, axis, pairs + [(j, i) for i, j in pairs]))  7.2 us
    pallas_call x1, Pallas kernels, shards(): pl.pallas_call(functools.partial(spectrum_body, extent=extent, dims=dims,...  6.45 us
    ppermute x5, waiting for transfers between devices, all_max(): moved.append(lax.ppermute(value, axis, pairs))  4.09 us
    max x5, other arithmetic, all_max(): jnp.maximum(value, new)  3.97 us
    reshape x1, local copies, waits for them, and re-layouts, shards(): point_spread.reshape(extent * extent, extent)  1.89 us
  transfers between devices with their start and end apart: 19, of which 8 were waited for; matrix products, arithmetic and copies ran while one was open for 7% of the time, Pallas kernels for 7%

profile of v1, /device:TPU:0, one launch (start us, length us, event | category | flops | bytes accessed | tf_op | source)
XLA Modules:
  0.0 90.8 jit_solution(10182584958487845898)
XLA Ops:
  0.6 1.6 %shard_map.174 = f32[64,128]{1,0:T(8,128)} custom-call(f32[256,128]{1,0:T(8,128)} %bitcast.5), custom_call_target="tpu_custom_call" | custom-call | tf_op jit(solution)/shard_map/pallas_call | solution.py:311
  2.9 5.9 %collective-permute-start = (f32[64,128]{1,0:T(8,128)}, f32[64,128]{1,0:T(8,128)S(1)}, u32[]{:S(2)}, u32[]{:S(2)}) collective-permute-start(f32[64,128]{1,0:T(8,128)} %shard_map.174), channel_id=1, source_target_pairs={{0,2},{4,6},{2,0},{6,4},{1,3},{5,7},{3,1},{7,5},{8,10},{12,14},{10... | collective-permute-start | bytes 98312 | tf_op jit(solution)/shard_map/ppermute | solution.py:228
  8.9 2.1 %collective-permute-done = f32[64,128]{1,0:T(8,128)S(1)} collective-permute-done((f32[64,128]{1,0:T(8,128)}, f32[64,128]{1,0:T(8,128)S(1)}, u32[]{:S(2)}, u32[]{:S(2)}) %collective-permute-start) | collective-permute-done | bytes 32800 | tf_op jit(solution)/shard_map/ppermute | solution.py:228
  11.9 1.6 %collective-permute-start.4 = (f32[320,128]{1,0:T(8,128)S(1)}, f32[320,128]{1,0:T(8,128)S(1)}, u32[]{:S(2)}, u32[]{:S(2)}) collective-permute-start(f32[320,128]{1,0:T(8,128)S(1)} %pad_maximum_fusion.refs_0_), channel_id=1, source_target_pairs={{0,1},{1,0},{2,3},{3,2},{4,5},{5,4},{6,7},{7,6},{8,9},{9,8},{10,11... | collective-permute-start | bytes 491528 | tf_op jit(solution)/shard_map/ppermute | solution.py:228
  14.1 2.9 %collective-permute-start.2 = (f32[320,128]{1,0:T(8,128)S(1)}, f32[320,128]{1,0:T(8,128)S(1)}, u32[]{:S(2)}, u32[]{:S(2)}) collective-permute-start(f32[320,128]{1,0:T(8,128)S(1)} %pad_maximum_fusion.refs_0_), channel_id=1, source_target_pairs={{0,8},{16,24},{8,0},{24,16},{1,9},{17,25},{9,1},{25,17},{2,10},{18... | collective-permute-start | bytes 491528 | tf_op jit(solution)/shard_map/ppermute | solution.py:228
  17.9 2.9 %collective-permute-start.5 = (f32[320,128]{1,0:T(8,128)S(1)}, f32[320,128]{1,0:T(8,128)S(1)}, u32[]{:S(2)}, u32[]{:S(2)}) collective-permute-start(f32[320,128]{1,0:T(8,128)S(1)} %collective-permute-done.4.refs_3_), channel_id=1, source_target_pairs={{0,8},{16,24},{8,0},{24,16},{1,9},{17,25},{9,1},{25,17},{2,10},{18... | collective-permute-start | bytes 491528 | tf_op jit(solution)/shard_map/ppermute | solution.py:228
  20.9 1.9 %reshape.22.psf = f32[1024,32]{1,0:T(8,128)} reshape(f32[32,1024]{1,0:T(8,128)} %param.17) | data formatting | bytes 262144 | tf_op jit(solution)/shard_map/reshape | solution.py:318
  22.7 6.5 %shard_map.175.refs_7_ = f32[4608,128]{1,0:T(8,128)} custom-call(f32[1024,32]{1,0:T(8,128)} %reshape.22.psf, bf16[32,256]{1,0:T(8,128)(2,1)} %constant.87.clone.ty_h, bf16[32,256]{1,0:T(8,128)(2,1)} %constant.88.clone.ty_l, bf16[192,64]{1,0:T(8,128)(2,1)} %constant.89.clone.fx.fz, bf16[192,64]{1,0:T(8,128)(2,1)} %constant.89.clone.fx.fz), custom_call_target="tpu_custom_call" | custom-call | tf_op jit(solution)/shard_map/pallas_call | solution.py:314
  30.7 12.3 %shard_map.176 = (f32[256,128]{1,0:T(8,128)}, f32[64,128]{1,0:T(8,128)}) custom-call(s32[2]{0:T(128)} %pad_add_fusion.place, f32[320,128]{1,0:T(8,128)} %copy-done, f32[320,128]{1,0:T(8,128)} %copy-done.4, f32[320,128]{1,0:T(8,128)} %copy-done.3, f32[320,128]{1,0:T(8,128)} %copy-done.2, f32[320,128]{1,0:T(8,128)} %copy-done.6, f32[320,128]{1,0:T(8,128)} %copy-done.5, ...), custom_call_target="tpu_custom_call" | custom-call | tf_op jit(solution)/shard_map/pallas_call | solution.py:321
  43.7 3.8 %collective-permute-start.7 = (f32[64,128]{1,0:T(8,128)}, f32[64,128]{1,0:T(8,128)S(1)}, u32[]{:S(2)}, u32[]{:S(2)}) collective-permute-start(f32[64,128]{1,0:T(8,128)} %get-tuple-element.11), channel_id=1, source_target_pairs={{0,2},{4,6},{2,0},{6,4},{1,3},{5,7},{3,1},{7,5},{8,10},{12,14},{10... | collective-permute-start | bytes 98312 | tf_op jit(solution)/shard_map/ppermute | solution.py:228
  47.5 2.1 %collective-permute-done.7 = f32[64,128]{1,0:T(8,128)S(1)} collective-permute-done((f32[64,128]{1,0:T(8,128)}, f32[64,128]{1,0:T(8,128)S(1)}, u32[]{:S(2)}, u32[]{:S(2)}) %collective-permute-start.7) | collective-permute-done | bytes 32800 | tf_op jit(solution)/shard_map/ppermute | solution.py:228
  50.5 1.6 %collective-permute-start.11 = (f32[320,128]{1,0:T(8,128)S(1)}, f32[320,128]{1,0:T(8,128)S(1)}, u32[]{:S(2)}, u32[]{:S(2)}) collective-permute-start(f32[320,128]{1,0:T(8,128)S(1)} %pad_maximum_fusion.1.refs_0_), channel_id=1, source_target_pairs={{0,1},{1,0},{2,3},{3,2},{4,5},{5,4},{6,7},{7,6},{8,9},{9,8},{10,11... | collective-permute-start | bytes 491528 | tf_op jit(solution)/shard_map/ppermute | solution.py:228
  52.8 1.3 %collective-permute-start.9 = (f32[320,128]{1,0:T(8,128)S(1)}, f32[320,128]{1,0:T(8,128)S(1)}, u32[]{:S(2)}, u32[]{:S(2)}) collective-permute-start(f32[320,128]{1,0:T(8,128)S(1)} %pad_maximum_fusion.1.refs_0_), channel_id=1, source_target_pairs={{0,8},{16,24},{8,0},{24,16},{1,9},{17,25},{9,1},{25,17},{2,10},{18... | collective-permute-start | bytes 491528 | tf_op jit(solution)/shard_map/ppermute | solution.py:228
  54.1 1.8 %collective-permute-done.11.refs_3_ = f32[320,128]{1,0:T(8,128)S(1)} collective-permute-done((f32[320,128]{1,0:T(8,128)S(1)}, f32[320,128]{1,0:T(8,128)S(1)}, u32[]{:S(2)}, u32[]{:S(2)}) %collective-permute-start.11) | collective-permute-done | bytes 163872 | tf_op jit(solution)/shard_map/ppermute | solution.py:228
  56.6 1.5 %collective-permute-start.12 = (f32[320,128]{1,0:T(8,128)S(1)}, f32[320,128]{1,0:T(8,128)S(1)}, u32[]{:S(2)}, u32[]{:S(2)}) collective-permute-start(f32[320,128]{1,0:T(8,128)S(1)} %collective-permute-done.11.refs_3_), channel_id=1, source_target_pairs={{0,8},{16,24},{8,0},{24,16},{1,9},{17,25},{9,1},{25,17},{2,10},{18... | collective-permute-start | bytes 491528 | tf_op jit(solution)/shard_map/ppermute | solution.py:228
  59.8 12.3 %shard_map.177 = (f32[256,128]{1,0:T(8,128)}, f32[16,128]{1,0:T(8,128)}, f32[16,128]{1,0:T(8,128)}, f32[16,16]{1,0:T(8,128)}) custom-call(s32[2]{0:T(128)} %pad_add_fusion.place, f32[320,128]{1,0:T(8,128)} %copy-done.1, f32[320,128]{1,0:T(8,128)} %copy-done.9, f32[320,128]{1,0:T(8,128)} %copy-done.8, f32[320,128]{1,0:T(8,128)} %copy-done.7, ...), custom_call_target="tpu_custom_call" | custom-call | tf_op jit(solution)/shard_map/pallas_call | solution.py:321
  72.0 2.6 %collective-permute-start.14 = (f32[16,128]{1,0:T(8,128)}, f32[16,128]{1,0:T(8,128)S(1)}, u32[]{:S(2)}, u32[]{:S(2)}) collective-permute-start(f32[16,128]{1,0:T(8,128)} %get-tuple-element.13), channel_id=1, source_target_pairs={{0,8},{8,0},{16,24},{24,16},{1,9},{9,1},{17,25},{25,17},{2,10},{10... | collective-permute-start | bytes 24584 | tf_op jit(solution)/shard_map/ppermute | solution.py:263
  74.6 1.5 %collective-permute-start.18 = (f32[16,128]{1,0:T(8,128)}, f32[16,128]{1,0:T(8,128)S(1)}, u32[]{:S(2)}, u32[]{:S(2)}) collective-permute-start(f32[16,128]{1,0:T(8,128)} %get-tuple-element.15), channel_id=1, source_target_pairs={{0,1},{1,0},{2,3},{3,2},{4,5},{5,4},{6,7},{7,6},{8,9},{9,8},{10,11... | collective-permute-start | bytes 24584 | tf_op jit(solution)/shard_map/ppermute | solution.py:263
  76.2 2.0 %collective-permute-start.16 = (f32[16,16]{1,0:T(8,128)}, f32[16,16]{1,0:T(8,128)S(1)}, u32[]{:S(2)}, u32[]{:S(2)}) collective-permute-start(f32[16,16]{1,0:T(8,128)} %get-tuple-element.14), channel_id=1, source_target_pairs={{0,2},{2,0},{4,6},{6,4},{1,3},{3,1},{5,7},{7,5},{8,10},{10,8},{12,... | collective-permute-start | bytes 3080 | tf_op jit(solution)/shard_map/ppermute | solution.py:263
  78.2 1.8 %collective-permute-done.16 = f32[16,16]{1,0:T(8,128)S(1)} collective-permute-done((f32[16,16]{1,0:T(8,128)}, f32[16,16]{1,0:T(8,128)S(1)}, u32[]{:S(2)}, u32[]{:S(2)}) %collective-permute-start.16) | collective-permute-done | bytes 1056 | tf_op jit(solution)/shard_map/ppermute | solution.py:263
  80.7 2.9 %collective-permute-start.17 = (f32[16,16]{1,0:T(8,128)S(1)}, f32[16,16]{1,0:T(8,128)S(1)}, u32[]{:S(2)}, u32[]{:S(2)}) collective-permute-start(f32[16,16]{1,0:T(8,128)S(1)} %max.18), channel_id=1, source_target_pairs={{0,4},{2,6},{4,0},{6,2},{1,5},{3,7},{5,1},{7,3},{8,12},{10,14},{12... | collective-permute-start | bytes 3080 | tf_op jit(solution)/shard_map/ppermute | solution.py:263
  83.6 1.7 %collective-permute-done.17 = f32[16,16]{1,0:T(8,128)S(1)} collective-permute-done((f32[16,16]{1,0:T(8,128)S(1)}, f32[16,16]{1,0:T(8,128)S(1)}, u32[]{:S(2)}, u32[]{:S(2)}) %collective-permute-start.17) | collective-permute-done | bytes 1056 | tf_op jit(solution)/shard_map/ppermute | solution.py:263
  86.6 1.7 %collective-permute-start.15 = (f32[16,128]{1,0:T(8,128)S(1)}, f32[16,128]{1,0:T(8,128)S(1)}, u32[]{:S(2)}, u32[]{:S(2)}) collective-permute-start(f32[16,128]{1,0:T(8,128)S(1)} %max.16), channel_id=1, source_target_pairs={{0,16},{8,24},{16,0},{24,8},{1,17},{9,25},{17,1},{25,9},{2,18},{10... | collective-permute-start | bytes 24584 | tf_op jit(solution)/shard_map/ppermute | solution.py:263
  88.3 1.4 %dynamic-slice_maximum_fusion = f32[16,64]{1,0:T(8,128)} fusion(f32[16,128]{1,0:T(8,128)S(1)} %collective-permute-done.18, s32[]{:T(128)S(6)} %select_n.41, f32[16,128]{1,0:T(8,128)} %get-tuple-element.15), kind=kLoop, calls=%fused_computation.6 | loop fusion | flops 1024 | bytes 12292 | tf_op jit(solution)/shard_map/max | solution.py:266
  (56 shorter events, 12.4 us)
Async XLA Ops:
  2.3 6.6 %collective-permute-start.1 = (f32[64,128]{1,0:T(8,128)}, f32[64,128]{1,0:T(8,128)S(1)}, u32[]{:S(2)}, u32[]{:S(2)}) collective-permute-start(f32[64,128]{1,0:T(8,128)} %shard_map.174), channel_id=1, source_target_pairs={{2,4},{4,2},{3,5},{5,3},{10,12},{12,10},{11,13},{13,11},{18,20},{2... | collective-permute-start | bytes 98312 | tf_op jit(solution)/shard_map/ppermute | solution.py:228
  2.9 8.0 %collective-permute-start = (f32[64,128]{1,0:T(8,128)}, f32[64,128]{1,0:T(8,128)S(1)}, u32[]{:S(2)}, u32[]{:S(2)}) collective-permute-start(f32[64,128]{1,0:T(8,128)} %shard_map.174), channel_id=1, source_target_pairs={{0,2},{4,6},{2,0},{6,4},{1,3},{5,7},{3,1},{7,5},{8,10},{12,14},{10... | collective-permute-start | bytes 98312 | tf_op jit(solution)/shard_map/ppermute | solution.py:228
  11.9 18.0 %copy-start = (f32[320,128]{1,0:T(8,128)}, f32[320,128]{1,0:T(8,128)S(1)}, u32[]{:S(2)}) copy-start(f32[320,128]{1,0:T(8,128)S(1)} %pad_maximum_fusion.refs_0_) | copy-start | bytes 491524
  11.9 5.4 %collective-permute-start.4 = (f32[320,128]{1,0:T(8,128)S(1)}, f32[320,128]{1,0:T(8,128)S(1)}, u32[]{:S(2)}, u32[]{:S(2)}) collective-permute-start(f32[320,128]{1,0:T(8,128)S(1)} %pad_maximum_fusion.refs_0_), channel_id=1, source_target_pairs={{0,1},{1,0},{2,3},{3,2},{4,5},{5,4},{6,7},{7,6},{8,9},{9,8},{10,11... | collective-permute-start | bytes 491528 | tf_op jit(solution)/shard_map/ppermute | solution.py:228
  13.5 16.4 %collective-permute-start.3 = (f32[320,128]{1,0:T(8,128)S(1)}, f32[320,128]{1,0:T(8,128)S(1)}, u32[]{:S(2)}, u32[]{:S(2)}) collective-permute-start(f32[320,128]{1,0:T(8,128)S(1)} %pad_maximum_fusion.refs_0_), channel_id=1, source_target_pairs={{8,16},{16,8},{9,17},{17,9},{10,18},{18,10},{11,19},{19,11},{12,20... | collective-permute-start | bytes 491528 | tf_op jit(solution)/shard_map/ppermute | solution.py:228
  14.1 15.7 %collective-permute-start.2 = (f32[320,128]{1,0:T(8,128)S(1)}, f32[320,128]{1,0:T(8,128)S(1)}, u32[]{:S(2)}, u32[]{:S(2)}) collective-permute-start(f32[320,128]{1,0:T(8,128)S(1)} %pad_maximum_fusion.refs_0_), channel_id=1, source_target_pairs={{0,8},{16,24},{8,0},{24,16},{1,9},{17,25},{9,1},{25,17},{2,10},{18... | collective-permute-start | bytes 491528 | tf_op jit(solution)/shard_map/ppermute | solution.py:228
  17.3 12.7 %copy-start.2 = (f32[320,128]{1,0:T(8,128)}, f32[320,128]{1,0:T(8,128)S(1)}, u32[]{:S(2)}) copy-start(f32[320,128]{1,0:T(8,128)S(1)} %collective-permute-done.4.refs_3_) | copy-start | bytes 491524
  17.3 12.6 %collective-permute-start.6 = (f32[320,128]{1,0:T(8,128)S(1)}, f32[320,128]{1,0:T(8,128)S(1)}, u32[]{:S(2)}, u32[]{:S(2)}) collective-permute-start(f32[320,128]{1,0:T(8,128)S(1)} %collective-permute-done.4.refs_3_), channel_id=1, source_target_pairs={{8,16},{16,8},{9,17},{17,9},{10,18},{18,10},{11,19},{19,11},{12,20... | collective-permute-start | bytes 491528 | tf_op jit(solution)/shard_map/ppermute | solution.py:228
  17.9 12.0 %collective-permute-start.5 = (f32[320,128]{1,0:T(8,128)S(1)}, f32[320,128]{1,0:T(8,128)S(1)}, u32[]{:S(2)}, u32[]{:S(2)}) collective-permute-start(f32[320,128]{1,0:T(8,128)S(1)} %collective-permute-done.4.refs_3_), channel_id=1, source_target_pairs={{0,8},{16,24},{8,0},{24,16},{1,9},{17,25},{9,1},{25,17},{2,10},{18... | collective-permute-start | bytes 491528 | tf_op jit(solution)/shard_map/ppermute | solution.py:228
  43.0 4.4 %collective-permute-start.8 = (f32[64,128]{1,0:T(8,128)}, f32[64,128]{1,0:T(8,128)S(1)}, u32[]{:S(2)}, u32[]{:S(2)}) collective-permute-start(f32[64,128]{1,0:T(8,128)} %get-tuple-element.11), channel_id=1, source_target_pairs={{2,4},{4,2},{3,5},{5,3},{10,12},{12,10},{11,13},{13,11},{18,20},{2... | collective-permute-start | bytes 98312 | tf_op jit(solution)/shard_map/ppermute | solution.py:228
  43.7 5.9 %collective-permute-start.7 = (f32[64,128]{1,0:T(8,128)}, f32[64,128]{1,0:T(8,128)S(1)}, u32[]{:S(2)}, u32[]{:S(2)}) collective-permute-start(f32[64,128]{1,0:T(8,128)} %get-tuple-element.11), channel_id=1, source_target_pairs={{0,2},{4,6},{2,0},{6,4},{1,3},{5,7},{3,1},{7,5},{8,10},{12,14},{10... | collective-permute-start | bytes 98312 | tf_op jit(solution)/shard_map/ppermute | solution.py:228
  50.5 8.6 %copy-start.1 = (f32[320,128]{1,0:T(8,128)}, f32[320,128]{1,0:T(8,128)S(1)}, u32[]{:S(2)}) copy-start(f32[320,128]{1,0:T(8,128)S(1)} %pad_maximum_fusion.1.refs_0_) | copy-start | bytes 491524
  50.5 5.4 %collective-permute-start.11 = (f32[320,128]{1,0:T(8,128)S(1)}, f32[320,128]{1,0:T(8,128)S(1)}, u32[]{:S(2)}, u32[]{:S(2)}) collective-permute-start(f32[320,128]{1,0:T(8,128)S(1)} %pad_maximum_fusion.1.refs_0_), channel_id=1, source_target_pairs={{0,1},{1,0},{2,3},{3,2},{4,5},{5,4},{6,7},{7,6},{8,9},{9,8},{10,11... | collective-permute-start | bytes 491528 | tf_op jit(solution)/shard_map/ppermute | solution.py:228
  52.1 5.9 %collective-permute-start.10 = (f32[320,128]{1,0:T(8,128)S(1)}, f32[320,128]{1,0:T(8,128)S(1)}, u32[]{:S(2)}, u32[]{:S(2)}) collective-permute-start(f32[320,128]{1,0:T(8,128)S(1)} %pad_maximum_fusion.1.refs_0_), channel_id=1, source_target_pairs={{8,16},{16,8},{9,17},{17,9},{10,18},{18,10},{11,19},{19,11},{12,20... | collective-permute-start | bytes 491528 | tf_op jit(solution)/shard_map/ppermute | solution.py:228
  52.8 5.3 %collective-permute-start.9 = (f32[320,128]{1,0:T(8,128)S(1)}, f32[320,128]{1,0:T(8,128)S(1)}, u32[]{:S(2)}, u32[]{:S(2)}) collective-permute-start(f32[320,128]{1,0:T(8,128)S(1)} %pad_maximum_fusion.1.refs_0_), channel_id=1, source_target_pairs={{0,8},{16,24},{8,0},{24,16},{1,9},{17,25},{9,1},{25,17},{2,10},{18... | collective-permute-start | bytes 491528 | tf_op jit(solution)/shard_map/ppermute | solution.py:228
  55.9 3.2 %copy-start.7 = (f32[320,128]{1,0:T(8,128)}, f32[320,128]{1,0:T(8,128)S(1)}, u32[]{:S(2)}) copy-start(f32[320,128]{1,0:T(8,128)S(1)} %collective-permute-done.11.refs_3_) | copy-start | bytes 491524
  55.9 2.2 %collective-permute-start.13 = (f32[320,128]{1,0:T(8,128)S(1)}, f32[320,128]{1,0:T(8,128)S(1)}, u32[]{:S(2)}, u32[]{:S(2)}) collective-permute-start(f32[320,128]{1,0:T(8,128)S(1)} %collective-permute-done.11.refs_3_), channel_id=1, source_target_pairs={{8,16},{16,8},{9,17},{17,9},{10,18},{18,10},{11,19},{19,11},{12,20... | collective-permute-start | bytes 491528 | tf_op jit(solution)/shard_map/ppermute | solution.py:228
  56.6 2.5 %collective-permute-start.12 = (f32[320,128]{1,0:T(8,128)S(1)}, f32[320,128]{1,0:T(8,128)S(1)}, u32[]{:S(2)}, u32[]{:S(2)}) collective-permute-start(f32[320,128]{1,0:T(8,128)S(1)} %collective-permute-done.11.refs_3_), channel_id=1, source_target_pairs={{0,8},{16,24},{8,0},{24,16},{1,9},{17,25},{9,1},{25,17},{2,10},{18... | collective-permute-start | bytes 491528 | tf_op jit(solution)/shard_map/ppermute | solution.py:228
  58.0 1.0 %copy-start.8 = (f32[320,128]{1,0:T(8,128)}, f32[320,128]{1,0:T(8,128)S(1)}, u32[]{:S(2)}) copy-start(f32[320,128]{1,0:T(8,128)S(1)} %collective-permute-done.10.refs_2_) | copy-start | bytes 491524
  72.0 13.8 %collective-permute-start.14 = (f32[16,128]{1,0:T(8,128)}, f32[16,128]{1,0:T(8,128)S(1)}, u32[]{:S(2)}, u32[]{:S(2)}) collective-permute-start(f32[16,128]{1,0:T(8,128)} %get-tuple-element.13), channel_id=1, source_target_pairs={{0,8},{8,0},{16,24},{24,16},{1,9},{9,1},{17,25},{25,17},{2,10},{10... | collective-permute-start | bytes 24584 | tf_op jit(solution)/shard_map/ppermute | solution.py:263
  74.6 13.7 %collective-permute-start.18 = (f32[16,128]{1,0:T(8,128)}, f32[16,128]{1,0:T(8,128)S(1)}, u32[]{:S(2)}, u32[]{:S(2)}) collective-permute-start(f32[16,128]{1,0:T(8,128)} %get-tuple-element.15), channel_id=1, source_target_pairs={{0,1},{1,0},{2,3},{3,2},{4,5},{5,4},{6,7},{7,6},{8,9},{9,8},{10,11... | collective-permute-start | bytes 24584 | tf_op jit(solution)/shard_map/ppermute | solution.py:263
  76.2 3.9 %collective-permute-start.16 = (f32[16,16]{1,0:T(8,128)}, f32[16,16]{1,0:T(8,128)S(1)}, u32[]{:S(2)}, u32[]{:S(2)}) collective-permute-start(f32[16,16]{1,0:T(8,128)} %get-tuple-element.14), channel_id=1, source_target_pairs={{0,2},{2,0},{4,6},{6,4},{1,3},{3,1},{5,7},{7,5},{8,10},{10,8},{12,... | collective-permute-start | bytes 3080 | tf_op jit(solution)/shard_map/ppermute | solution.py:263
  80.7 4.5 %collective-permute-start.17 = (f32[16,16]{1,0:T(8,128)S(1)}, f32[16,16]{1,0:T(8,128)S(1)}, u32[]{:S(2)}, u32[]{:S(2)}) collective-permute-start(f32[16,16]{1,0:T(8,128)S(1)} %max.18), channel_id=1, source_target_pairs={{0,4},{2,6},{4,0},{6,2},{1,5},{3,7},{5,1},{7,3},{8,12},{10,14},{12... | collective-permute-start | bytes 3080 | tf_op jit(solution)/shard_map/ppermute | solution.py:263
  86.6 3.7 %collective-permute-start.15 = (f32[16,128]{1,0:T(8,128)S(1)}, f32[16,128]{1,0:T(8,128)S(1)}, u32[]{:S(2)}, u32[]{:S(2)}) collective-permute-start(f32[16,128]{1,0:T(8,128)S(1)} %max.16), channel_id=1, source_target_pairs={{0,16},{8,24},{16,0},{24,8},{1,17},{9,25},{17,1},{25,9},{2,18},{10... | collective-permute-start | bytes 24584 | tf_op jit(solution)/shard_map/ppermute | solution.py:263
  (7 other events, 5.7 us)

commit v2 on v1

--- a/solution.py
+++ b/solution.py
@@ -10,6 +10,7 @@
 
 F32 = jnp.float32
 BF16 = jnp.bfloat16
+UNROLL = 8
 
 
 def split(value):
@@ -104,31 +105,40 @@
             s2[pl.ds((z + j) * 2 * length_x, 2 * length_x), :] = out[:, j * lanes : (j + 1) * lanes]
         return carry
 
-    lax.fori_loop(0, count_z // 2, step, 0, unroll=4)
+    lax.fori_loop(0, count_z // 2, step, 0, unroll=UNROLL)
 
 
 def spectrum_body(psf, ty_h, ty_l, fx, fz, spec, s1, s2, *, extent, dims, lanes):
     length_z, length_x, length_y = dims
+    width = ty_h.shape[1]
+    per = width // extent
+    tiles = extent // per
     values = psf[...]
     scale = 1.0 / (jnp.sum(values) * float(length_z * length_x * length_y))
-    s1[...] = dot_table(values, ty_h[...], ty_l[...]) * scale
-    transform_x(s1, s2, fx[...], extent, extent, length_x, lanes)
-    table = fz[...]
+    data = jnp.concatenate([values[:, t * width : (t + 1) * width] for t in range(tiles)], axis=0)
+    for g in range(per):
+        out = dot_table(data, ty_h[g], ty_l[g]) * scale
+        for t in range(tiles):
+            s1[pl.ds((t * per + g) * extent, extent), :] = out[t * extent : (t + 1) * extent]
+    transform_x(s1, s2, fz[...], extent, extent, length_z, lanes)
+    table = fx[...]
 
     def step(i, carry):
-        k = i * 2
-        data = jnp.concatenate(
-            [pair_strided(s2, k + j, length_x, extent, 2 * length_x) for j in range(2)], axis=1
+        q = i * 2
+        data = jnp.concatenate(
+            [pair_strided(s2, q + j, length_z, extent, 2 * length_z) for j in range(2)], axis=1
         )
         out = table_dot(table, data)
         for j in range(2):
-            spec[pl.ds((k + j) * 2 * length_z, 2 * length_z), :] = out[:, j * lanes : (j + 1) * lanes]
+            part = out[:, j * lanes : (j + 1) * lanes]
+            spec[pl.ds(q + j, length_x, stride=2 * length_z), :] = part[:length_x]
+            spec[pl.ds(length_z + q + j, length_x, stride=2 * length_z), :] = part[length_x:]
         return carry
 
-    lax.fori_loop(0, length_x // 2, step, 0, unroll=4)
-
-
-def conv_body(place, *refs, brick, dims, lanes, groups, parts, conj):
+    lax.fori_loop(0, length_z // 2, step, 0, unroll=UNROLL)
+
+
+def conv_body(*refs, brick, dims, lanes, groups, parts, conj):
     parts_z, parts_x = parts
     count = parts_z * parts_x
     region, refs = refs[:count], refs[count:]
@@ -155,8 +165,8 @@
                 z = bz * brick_z + g * per + zi
                 src = n * chunk + zi * brick_x
                 s1[pl.ds(z * wide_x + bx * brick_x, brick_x), :] = out[src : src + brick_x]
-    transform_x(s1, s2, fx[place[0]], wide_z, wide_x, length_x, lanes)
-    forward_z = fz[place[1]]
+    transform_x(s1, s2, fx[lax.axis_index("gx") % 2], wide_z, wide_x, length_x, lanes)
+    forward_z = fz[lax.axis_index("gz") % 2]
     back_z = gz[...]
 
     def middle(i, carry):
@@ -179,7 +189,7 @@
             s3[pl.ds((k + j) * 2 * brick_z, 2 * brick_z), :] = back[:, j * lanes : (j + 1) * lanes]
         return carry
 
-    lax.fori_loop(0, length_x // 2, middle, 0, unroll=4)
+    lax.fori_loop(0, length_x // 2, middle, 0, unroll=UNROLL)
     back_x = gx[...]
     for z in range(0, brick_z, 2):
         data = jnp.concatenate(
@@ -298,12 +308,15 @@
         *map(jnp.asarray, constant(inverse_right(length_y, inner(brick_y), lanes))),
     )
     offsets = np.arange(extent) - margin
+    per = max(1, 128 // extent)
+    psf_y = np.zeros((per, per * extent, 2 * lanes))
+    for g in range(per):
+        psf_y[g, g * extent : (g + 1) * extent] = forward_right(length_y, offsets, lanes)
     psf_tables = (
-        *map(jnp.asarray, constant(forward_right(length_y, offsets, lanes))),
+        *map(jnp.asarray, constant(psf_y)),
         stacked(forward_left(length_x, offsets)),
         stacked(forward_left(length_z, offsets)),
     )
-    place = jnp.stack([lax.axis_index("gx") % 2, lax.axis_index("gz") % 2]).astype(jnp.int32)
     shape = jax.ShapeDtypeStruct
     scratch = lambda *s: pltpu.VMEM(s, F32)
 
@@ -315,21 +328,19 @@
         functools.partial(spectrum_body, extent=extent, dims=dims, lanes=lanes),
         out_shape=shape((length_x * 2 * length_z, lanes), F32),
         scratch_shapes=[scratch(extent * extent, 2 * lanes), scratch(extent * 2 * length_x, lanes)],
-    )(point_spread.reshape(extent * extent, extent), *psf_tables)
+    )(point_spread, *psf_tables)
 
     def convolve(region, mate, conj, out_shape):
         return pl.pallas_call(
             functools.partial(conv_body, brick=brick, dims=dims, lanes=lanes, groups=groups, parts=parts, conj=conj),
             out_shape=out_shape,
-            in_specs=[pl.BlockSpec(memory_space=pltpu.SMEM)]
-            + [pl.BlockSpec(memory_space=pltpu.VMEM)] * (len(region) + 2 + len(conv_tables)),
             scratch_shapes=[
                 scratch(parts_z * brick_z * parts_x * brick_x, 2 * lanes),
                 scratch(parts_z * brick_z * 2 * length_x, lanes),
                 scratch(length_x * 2 * brick_z, lanes),
                 scratch(rows, 2 * lanes),
             ],
-        )(place, *region, mate, spec, *conv_tables)
+        )(*region, mate, spec, *conv_tables)
 
     ratio, ratio_edges = convolve(
         surround(own, edges, margin),

time: 91.3 us -> 87.2 us (0.955)
  local copies, waits for them, and re-layouts: 3.36 us -> 1.47 us
  Pallas kernels: 32.7 us -> 31.1 us
    reshape x1 -> x0, local copies, waits for them, and re-layouts: 1.89 us -> none  [shards(): point_spread.reshape(extent * extent, extent)]
    pallas_call x2, Pallas kernels: 24.6 us -> 23 us  [convolve(): pl.pallas_call(functools.partial(conv_body, brick=brick, dims=dims, lanes...]
  transfers between devices with their start and end apart: 19 -> 19, of which waited for: 8 -> 8; matrix products, arithmetic and copies ran while one was open for 7% -> 4% of each run, Pallas kernels for 7% -> 7%
where the time goes in v2:
time: 87.2 us; the launch traced here: 86.7 us
  starting transfers between devices  36.2 us (42%)
  Pallas kernels  31.1 us (36%)
  waiting for transfers between devices  11.3 us (13%)
  other arithmetic  5.83 us (7%)
  local copies, waits for them, and re-layouts  1.47 us (2%)
    ppermute x14, starting transfers between devices, swaps(): found.append(lax.ppermute(value, axis, pairs + [(j, i) for i, j in pairs]))  25.4 us
    pallas_call x2, Pallas kernels, convolve(): pl.pallas_call(functools.partial(conv_body, brick=brick, dims=dims, lanes...  23 us
    ppermute x5, starting transfers between devices, all_max(): moved.append(lax.ppermute(value, axis, pairs))  10.7 us
    ppermute x14, waiting for transfers between devices, swaps(): found.append(lax.ppermute(value, axis, pairs + [(j, i) for i, j in pairs]))  7.2 us
    pallas_call x1, Pallas kernels, shards(): pl.pallas_call(functools.partial(spectrum_body, extent=extent, dims=dims,...  6.48 us
    ppermute x5, waiting for transfers between devices, all_max(): moved.append(lax.ppermute(value, axis, pairs))  4.08 us
    max x5, other arithmetic, all_max(): jnp.maximum(value, new)  3.97 us
    concatenate x2, other arithmetic, surround(): block = jnp.concatenate([value, halo], axis=0)  1.84 us
  transfers between devices with their start and end apart: 19, of which 8 were waited for; matrix products, arithmetic and copies ran while one was open for 4% of the time, Pallas kernels for 7%

profile of v2, /device:TPU:0, one launch (start us, length us, event | category | flops | bytes accessed | tf_op | source)
XLA Modules:
  0.0 86.7 jit_solution(9333349439937255632)
XLA Ops:
  0.6 1.6 %shard_map.174 = f32[64,128]{1,0:T(8,128)} custom-call(f32[256,128]{1,0:T(8,128)} %bitcast.3), custom_call_target="tpu_custom_call" | custom-call | tf_op jit(solution)/shard_map/pallas_call | solution.py:324
  2.9 5.9 %collective-permute-start = (f32[64,128]{1,0:T(8,128)}, f32[64,128]{1,0:T(8,128)S(1)}, u32[]{:S(2)}, u32[]{:S(2)}) collective-permute-start(f32[64,128]{1,0:T(8,128)} %shard_map.174), channel_id=1, source_target_pairs={{0,2},{4,6},{2,0},{6,4},{1,3},{5,7},{3,1},{7,5},{8,10},{12,14},{10... | collective-permute-start | bytes 98312 | tf_op jit(solution)/shard_map/ppermute | solution.py:238
  8.9 2.1 %collective-permute-done = f32[64,128]{1,0:T(8,128)S(1)} collective-permute-done((f32[64,128]{1,0:T(8,128)}, f32[64,128]{1,0:T(8,128)S(1)}, u32[]{:S(2)}, u32[]{:S(2)}) %collective-permute-start) | collective-permute-done | bytes 32800 | tf_op jit(solution)/shard_map/ppermute | solution.py:238
  11.9 1.6 %collective-permute-start.4 = (f32[320,128]{1,0:T(8,128)S(1)}, f32[320,128]{1,0:T(8,128)S(1)}, u32[]{:S(2)}, u32[]{:S(2)}) collective-permute-start(f32[320,128]{1,0:T(8,128)S(1)} %pad_maximum_fusion.refs_0_), channel_id=1, source_target_pairs={{0,1},{1,0},{2,3},{3,2},{4,5},{5,4},{6,7},{7,6},{8,9},{9,8},{10,11... | collective-permute-start | bytes 491528 | tf_op jit(solution)/shard_map/ppermute | solution.py:238
  14.1 2.9 %collective-permute-start.2 = (f32[320,128]{1,0:T(8,128)S(1)}, f32[320,128]{1,0:T(8,128)S(1)}, u32[]{:S(2)}, u32[]{:S(2)}) collective-permute-start(f32[320,128]{1,0:T(8,128)S(1)} %pad_maximum_fusion.refs_0_), channel_id=1, source_target_pairs={{0,8},{16,24},{8,0},{24,16},{1,9},{17,25},{9,1},{25,17},{2,10},{18... | collective-permute-start | bytes 491528 | tf_op jit(solution)/shard_map/ppermute | solution.py:238
  17.9 2.9 %collective-permute-start.5 = (f32[320,128]{1,0:T(8,128)S(1)}, f32[320,128]{1,0:T(8,128)S(1)}, u32[]{:S(2)}, u32[]{:S(2)}) collective-permute-start(f32[320,128]{1,0:T(8,128)S(1)} %collective-permute-done.4.refs_3_), channel_id=1, source_target_pairs={{0,8},{16,24},{8,0},{24,16},{1,9},{17,25},{9,1},{25,17},{2,10},{18... | collective-permute-start | bytes 491528 | tf_op jit(solution)/shard_map/ppermute | solution.py:238
  20.9 6.5 %shard_map.175.refs_7_ = f32[4608,128]{1,0:T(8,128)} custom-call(f32[32,1024]{1,0:T(8,128)} %psf.1, bf16[4,128,256]{2,1,0:T(8,128)(2,1)} %constant.76.clone.ty_h, bf16[4,128,256]{2,1,0:T(8,128)(2,1)} %constant.77.clone.ty_l, bf16[192,64]{1,0:T(8,128)(2,1)} %constant.78.clone.fx.fz, bf16[192,64]{1,0:T(8,128)(2,1)} %constant.78.clone.fx.fz), custom_call_target="tpu_custom_call" | custom-call | tf_op jit(solution)/shard_map/pallas_call | solution.py:327
  28.2 11.5 %shard_map.176 = (f32[256,128]{1,0:T(8,128)}, f32[64,128]{1,0:T(8,128)}) custom-call(f32[320,128]{1,0:T(8,128)} %copy-done.1, f32[320,128]{1,0:T(8,128)} %copy-done.7, f32[320,128]{1,0:T(8,128)} %copy-done.6, f32[320,128]{1,0:T(8,128)} %copy-done.4, f32[320,128]{1,0:T(8,128)} %copy-done.11, f32[320,128]{1,0:T(8,128)} %copy-done.10, f32[256,128]{1,0:T(8,128)} %bitcast.6, ...), custom_call_target="tpu_custom_call" | custom-call | tf_op jit(solution)/shard_map/pallas_call | solution.py:334
  40.4 3.8 %collective-permute-start.7 = (f32[64,128]{1,0:T(8,128)}, f32[64,128]{1,0:T(8,128)S(1)}, u32[]{:S(2)}, u32[]{:S(2)}) collective-permute-start(f32[64,128]{1,0:T(8,128)} %get-tuple-element.11), channel_id=1, source_target_pairs={{0,2},{4,6},{2,0},{6,4},{1,3},{5,7},{3,1},{7,5},{8,10},{12,14},{10... | collective-permute-start | bytes 98312 | tf_op jit(solution)/shard_map/ppermute | solution.py:238
  44.2 2.1 %collective-permute-done.7 = f32[64,128]{1,0:T(8,128)S(1)} collective-permute-done((f32[64,128]{1,0:T(8,128)}, f32[64,128]{1,0:T(8,128)S(1)}, u32[]{:S(2)}, u32[]{:S(2)}) %collective-permute-start.7) | collective-permute-done | bytes 32800 | tf_op jit(solution)/shard_map/ppermute | solution.py:238
  47.2 1.6 %collective-permute-start.11 = (f32[320,128]{1,0:T(8,128)S(1)}, f32[320,128]{1,0:T(8,128)S(1)}, u32[]{:S(2)}, u32[]{:S(2)}) collective-permute-start(f32[320,128]{1,0:T(8,128)S(1)} %pad_maximum_fusion.1.refs_0_), channel_id=1, source_target_pairs={{0,1},{1,0},{2,3},{3,2},{4,5},{5,4},{6,7},{7,6},{8,9},{9,8},{10,11... | collective-permute-start | bytes 491528 | tf_op jit(solution)/shard_map/ppermute | solution.py:238
  49.5 1.3 %collective-permute-start.9 = (f32[320,128]{1,0:T(8,128)S(1)}, f32[320,128]{1,0:T(8,128)S(1)}, u32[]{:S(2)}, u32[]{:S(2)}) collective-permute-start(f32[320,128]{1,0:T(8,128)S(1)} %pad_maximum_fusion.1.refs_0_), channel_id=1, source_target_pairs={{0,8},{16,24},{8,0},{24,16},{1,9},{17,25},{9,1},{25,17},{2,10},{18... | collective-permute-start | bytes 491528 | tf_op jit(solution)/shard_map/ppermute | solution.py:238
  50.8 1.8 %collective-permute-done.11.refs_3_ = f32[320,128]{1,0:T(8,128)S(1)} collective-permute-done((f32[320,128]{1,0:T(8,128)S(1)}, f32[320,128]{1,0:T(8,128)S(1)}, u32[]{:S(2)}, u32[]{:S(2)}) %collective-permute-start.11) | collective-permute-done | bytes 163872 | tf_op jit(solution)/shard_map/ppermute | solution.py:238
  53.3 1.5 %collective-permute-start.12 = (f32[320,128]{1,0:T(8,128)S(1)}, f32[320,128]{1,0:T(8,128)S(1)}, u32[]{:S(2)}, u32[]{:S(2)}) collective-permute-start(f32[320,128]{1,0:T(8,128)S(1)} %collective-permute-done.11.refs_3_), channel_id=1, source_target_pairs={{0,8},{16,24},{8,0},{24,16},{1,9},{17,25},{9,1},{25,17},{2,10},{18... | collective-permute-start | bytes 491528 | tf_op jit(solution)/shard_map/ppermute | solution.py:238
  54.8 1.0 %collective-permute-done.12.refs_4_ = f32[320,128]{1,0:T(8,128)S(1)} collective-permute-done((f32[320,128]{1,0:T(8,128)S(1)}, f32[320,128]{1,0:T(8,128)S(1)}, u32[]{:S(2)}, u32[]{:S(2)}) %collective-permute-start.12) | collective-permute-done | bytes 163872 | tf_op jit(solution)/shard_map/ppermute | solution.py:238
  56.5 11.5 %shard_map.177 = (f32[256,128]{1,0:T(8,128)}, f32[16,128]{1,0:T(8,128)}, f32[16,128]{1,0:T(8,128)}, f32[16,16]{1,0:T(8,128)}) custom-call(f32[320,128]{1,0:T(8,128)} %copy-done, f32[320,128]{1,0:T(8,128)} %copy-done.5, f32[320,128]{1,0:T(8,128)} %copy-done.3, f32[320,128]{1,0:T(8,128)} %copy-done.2, f32[320,128]{1,0:T(8,128)} %copy-done.9, ...), custom_call_target="tpu_custom_call" | custom-call | tf_op jit(solution)/shard_map/pallas_call | solution.py:334
  68.0 2.6 %collective-permute-start.14 = (f32[16,128]{1,0:T(8,128)}, f32[16,128]{1,0:T(8,128)S(1)}, u32[]{:S(2)}, u32[]{:S(2)}) collective-permute-start(f32[16,128]{1,0:T(8,128)} %get-tuple-element.13), channel_id=1, source_target_pairs={{0,8},{8,0},{16,24},{24,16},{1,9},{9,1},{17,25},{25,17},{2,10},{10... | collective-permute-start | bytes 24584 | tf_op jit(solution)/shard_map/ppermute | solution.py:273
  70.5 1.5 %collective-permute-start.18 = (f32[16,128]{1,0:T(8,128)}, f32[16,128]{1,0:T(8,128)S(1)}, u32[]{:S(2)}, u32[]{:S(2)}) collective-permute-start(f32[16,128]{1,0:T(8,128)} %get-tuple-element.15), channel_id=1, source_target_pairs={{0,1},{1,0},{2,3},{3,2},{4,5},{5,4},{6,7},{7,6},{8,9},{9,8},{10,11... | collective-permute-start | bytes 24584 | tf_op jit(solution)/shard_map/ppermute | solution.py:273
  72.1 2.0 %collective-permute-start.16 = (f32[16,16]{1,0:T(8,128)}, f32[16,16]{1,0:T(8,128)S(1)}, u32[]{:S(2)}, u32[]{:S(2)}) collective-permute-start(f32[16,16]{1,0:T(8,128)} %get-tuple-element.14), channel_id=1, source_target_pairs={{0,2},{2,0},{4,6},{6,4},{1,3},{3,1},{5,7},{7,5},{8,10},{10,8},{12,... | collective-permute-start | bytes 3080 | tf_op jit(solution)/shard_map/ppermute | solution.py:273
  74.1 1.8 %collective-permute-done.16 = f32[16,16]{1,0:T(8,128)S(1)} collective-permute-done((f32[16,16]{1,0:T(8,128)}, f32[16,16]{1,0:T(8,128)S(1)}, u32[]{:S(2)}, u32[]{:S(2)}) %collective-permute-start.16) | collective-permute-done | bytes 1056 | tf_op jit(solution)/shard_map/ppermute | solution.py:273
  76.6 2.9 %collective-permute-start.17 = (f32[16,16]{1,0:T(8,128)S(1)}, f32[16,16]{1,0:T(8,128)S(1)}, u32[]{:S(2)}, u32[]{:S(2)}) collective-permute-start(f32[16,16]{1,0:T(8,128)S(1)} %max.18), channel_id=1, source_target_pairs={{0,4},{2,6},{4,0},{6,2},{1,5},{3,7},{5,1},{7,3},{8,12},{10,14},{12... | collective-permute-start | bytes 3080 | tf_op jit(solution)/shard_map/ppermute | solution.py:273
  79.5 1.7 %collective-permute-done.17 = f32[16,16]{1,0:T(8,128)S(1)} collective-permute-done((f32[16,16]{1,0:T(8,128)S(1)}, f32[16,16]{1,0:T(8,128)S(1)}, u32[]{:S(2)}, u32[]{:S(2)}) %collective-permute-start.17) | collective-permute-done | bytes 1056 | tf_op jit(solution)/shard_map/ppermute | solution.py:273
  82.5 1.7 %collective-permute-start.15 = (f32[16,128]{1,0:T(8,128)S(1)}, f32[16,128]{1,0:T(8,128)S(1)}, u32[]{:S(2)}, u32[]{:S(2)}) collective-permute-start(f32[16,128]{1,0:T(8,128)S(1)} %max.16), channel_id=1, source_target_pairs={{0,16},{8,24},{16,0},{24,8},{1,17},{9,25},{17,1},{25,9},{2,18},{10... | collective-permute-start | bytes 24584 | tf_op jit(solution)/shard_map/ppermute | solution.py:273
  84.2 1.4 %dynamic-slice_maximum_fusion = f32[16,64]{1,0:T(8,128)} fusion(f32[16,128]{1,0:T(8,128)S(1)} %collective-permute-done.18, s32[]{:T(128)S(6)} %select_n.31, f32[16,128]{1,0:T(8,128)} %get-tuple-element.15), kind=kLoop, calls=%fused_computation.6 | loop fusion | flops 1024 | bytes 12292 | tf_op jit(solution)/shard_map/max | solution.py:276
  (54 shorter events, 10.7 us)
Async XLA Ops:
  2.3 6.6 %collective-permute-start.1 = (f32[64,128]{1,0:T(8,128)}, f32[64,128]{1,0:T(8,128)S(1)}, u32[]{:S(2)}, u32[]{:S(2)}) collective-permute-start(f32[64,128]{1,0:T(8,128)} %shard_map.174), channel_id=1, source_target_pairs={{2,4},{4,2},{3,5},{5,3},{10,12},{12,10},{11,13},{13,11},{18,20},{2... | collective-permute-start | bytes 98312 | tf_op jit(solution)/shard_map/ppermute | solution.py:238
  2.9 8.0 %collective-permute-start = (f32[64,128]{1,0:T(8,128)}, f32[64,128]{1,0:T(8,128)S(1)}, u32[]{:S(2)}, u32[]{:S(2)}) collective-permute-start(f32[64,128]{1,0:T(8,128)} %shard_map.174), channel_id=1, source_target_pairs={{0,2},{4,6},{2,0},{6,4},{1,3},{5,7},{3,1},{7,5},{8,10},{12,14},{10... | collective-permute-start | bytes 98312 | tf_op jit(solution)/shard_map/ppermute | solution.py:238
  11.9 15.5 %copy-start.1 = (f32[320,128]{1,0:T(8,128)}, f32[320,128]{1,0:T(8,128)S(1)}, u32[]{:S(2)}) copy-start(f32[320,128]{1,0:T(8,128)S(1)} %pad_maximum_fusion.refs_0_) | copy-start | bytes 491524
  11.9 5.4 %collective-permute-start.4 = (f32[320,128]{1,0:T(8,128)S(1)}, f32[320,128]{1,0:T(8,128)S(1)}, u32[]{:S(2)}, u32[]{:S(2)}) collective-permute-start(f32[320,128]{1,0:T(8,128)S(1)} %pad_maximum_fusion.refs_0_), channel_id=1, source_target_pairs={{0,1},{1,0},{2,3},{3,2},{4,5},{5,4},{6,7},{7,6},{8,9},{9,8},{10,11... | collective-permute-start | bytes 491528 | tf_op jit(solution)/shard_map/ppermute | solution.py:238
  13.5 13.9 %collective-permute-start.3 = (f32[320,128]{1,0:T(8,128)S(1)}, f32[320,128]{1,0:T(8,128)S(1)}, u32[]{:S(2)}, u32[]{:S(2)}) collective-permute-start(f32[320,128]{1,0:T(8,128)S(1)} %pad_maximum_fusion.refs_0_), channel_id=1, source_target_pairs={{8,16},{16,8},{9,17},{17,9},{10,18},{18,10},{11,19},{19,11},{12,20... | collective-permute-start | bytes 491528 | tf_op jit(solution)/shard_map/ppermute | solution.py:238
  14.1 13.2 %collective-permute-start.2 = (f32[320,128]{1,0:T(8,128)S(1)}, f32[320,128]{1,0:T(8,128)S(1)}, u32[]{:S(2)}, u32[]{:S(2)}) collective-permute-start(f32[320,128]{1,0:T(8,128)S(1)} %pad_maximum_fusion.refs_0_), channel_id=1, source_target_pairs={{0,8},{16,24},{8,0},{24,16},{1,9},{17,25},{9,1},{25,17},{2,10},{18... | collective-permute-start | bytes 491528 | tf_op jit(solution)/shard_map/ppermute | solution.py:238
  17.3 10.1 %copy-start.4 = (f32[320,128]{1,0:T(8,128)}, f32[320,128]{1,0:T(8,128)S(1)}, u32[]{:S(2)}) copy-start(f32[320,128]{1,0:T(8,128)S(1)} %collective-permute-done.4.refs_3_) | copy-start | bytes 491524
  17.3 10.1 %collective-permute-start.6 = (f32[320,128]{1,0:T(8,128)S(1)}, f32[320,128]{1,0:T(8,128)S(1)}, u32[]{:S(2)}, u32[]{:S(2)}) collective-permute-start(f32[320,128]{1,0:T(8,128)S(1)} %collective-permute-done.4.refs_3_), channel_id=1, source_target_pairs={{8,16},{16,8},{9,17},{17,9},{10,18},{18,10},{11,19},{19,11},{12,20... | collective-permute-start | bytes 491528 | tf_op jit(solution)/shard_map/ppermute | solution.py:238
  17.9 9.4 %collective-permute-start.5 = (f32[320,128]{1,0:T(8,128)S(1)}, f32[320,128]{1,0:T(8,128)S(1)}, u32[]{:S(2)}, u32[]{:S(2)}) collective-permute-start(f32[320,128]{1,0:T(8,128)S(1)} %collective-permute-done.4.refs_3_), channel_id=1, source_target_pairs={{0,8},{16,24},{8,0},{24,16},{1,9},{17,25},{9,1},{25,17},{2,10},{18... | collective-permute-start | bytes 491528 | tf_op jit(solution)/shard_map/ppermute | solution.py:238
  39.7 4.4 %collective-permute-start.8 = (f32[64,128]{1,0:T(8,128)}, f32[64,128]{1,0:T(8,128)S(1)}, u32[]{:S(2)}, u32[]{:S(2)}) collective-permute-start(f32[64,128]{1,0:T(8,128)} %get-tuple-element.11), channel_id=1, source_target_pairs={{2,4},{4,2},{3,5},{5,3},{10,12},{12,10},{11,13},{13,11},{18,20},{2... | collective-permute-start | bytes 98312 | tf_op jit(solution)/shard_map/ppermute | solution.py:238
  40.4 5.9 %collective-permute-start.7 = (f32[64,128]{1,0:T(8,128)}, f32[64,128]{1,0:T(8,128)S(1)}, u32[]{:S(2)}, u32[]{:S(2)}) collective-permute-start(f32[64,128]{1,0:T(8,128)} %get-tuple-element.11), channel_id=1, source_target_pairs={{0,2},{4,6},{2,0},{6,4},{1,3},{5,7},{3,1},{7,5},{8,10},{12,14},{10... | collective-permute-start | bytes 98312 | tf_op jit(solution)/shard_map/ppermute | solution.py:238
  47.2 8.6 %copy-start = (f32[320,128]{1,0:T(8,128)}, f32[320,128]{1,0:T(8,128)S(1)}, u32[]{:S(2)}) copy-start(f32[320,128]{1,0:T(8,128)S(1)} %pad_maximum_fusion.1.refs_0_) | copy-start | bytes 491524
  47.2 5.4 %collective-permute-start.11 = (f32[320,128]{1,0:T(8,128)S(1)}, f32[320,128]{1,0:T(8,128)S(1)}, u32[]{:S(2)}, u32[]{:S(2)}) collective-permute-start(f32[320,128]{1,0:T(8,128)S(1)} %pad_maximum_fusion.1.refs_0_), channel_id=1, source_target_pairs={{0,1},{1,0},{2,3},{3,2},{4,5},{5,4},{6,7},{7,6},{8,9},{9,8},{10,11... | collective-permute-start | bytes 491528 | tf_op jit(solution)/shard_map/ppermute | solution.py:238
  48.8 5.9 %collective-permute-start.10 = (f32[320,128]{1,0:T(8,128)S(1)}, f32[320,128]{1,0:T(8,128)S(1)}, u32[]{:S(2)}, u32[]{:S(2)}) collective-permute-start(f32[320,128]{1,0:T(8,128)S(1)} %pad_maximum_fusion.1.refs_0_), channel_id=1, source_target_pairs={{8,16},{16,8},{9,17},{17,9},{10,18},{18,10},{11,19},{19,11},{12,20... | collective-permute-start | bytes 491528 | tf_op jit(solution)/shard_map/ppermute | solution.py:238
  49.5 5.3 %collective-permute-start.9 = (f32[320,128]{1,0:T(8,128)S(1)}, f32[320,128]{1,0:T(8,128)S(1)}, u32[]{:S(2)}, u32[]{:S(2)}) collective-permute-start(f32[320,128]{1,0:T(8,128)S(1)} %pad_maximum_fusion.1.refs_0_), channel_id=1, source_target_pairs={{0,8},{16,24},{8,0},{24,16},{1,9},{17,25},{9,1},{25,17},{2,10},{18... | collective-permute-start | bytes 491528 | tf_op jit(solution)/shard_map/ppermute | solution.py:238
  52.6 3.2 %copy-start.2 = (f32[320,128]{1,0:T(8,128)}, f32[320,128]{1,0:T(8,128)S(1)}, u32[]{:S(2)}) copy-start(f32[320,128]{1,0:T(8,128)S(1)} %collective-permute-done.11.refs_3_) | copy-start | bytes 491524
  52.6 2.2 %collective-permute-start.13 = (f32[320,128]{1,0:T(8,128)S(1)}, f32[320,128]{1,0:T(8,128)S(1)}, u32[]{:S(2)}, u32[]{:S(2)}) collective-permute-start(f32[320,128]{1,0:T(8,128)S(1)} %collective-permute-done.11.refs_3_), channel_id=1, source_target_pairs={{8,16},{16,8},{9,17},{17,9},{10,18},{18,10},{11,19},{19,11},{12,20... | collective-permute-start | bytes 491528 | tf_op jit(solution)/shard_map/ppermute | solution.py:238
  53.3 2.5 %collective-permute-start.12 = (f32[320,128]{1,0:T(8,128)S(1)}, f32[320,128]{1,0:T(8,128)S(1)}, u32[]{:S(2)}, u32[]{:S(2)}) collective-permute-start(f32[320,128]{1,0:T(8,128)S(1)} %collective-permute-done.11.refs_3_), channel_id=1, source_target_pairs={{0,8},{16,24},{8,0},{24,16},{1,9},{17,25},{9,1},{25,17},{2,10},{18... | collective-permute-start | bytes 491528 | tf_op jit(solution)/shard_map/ppermute | solution.py:238
  54.8 1.0 %copy-start.3 = (f32[320,128]{1,0:T(8,128)}, f32[320,128]{1,0:T(8,128)S(1)}, u32[]{:S(2)}) copy-start(f32[320,128]{1,0:T(8,128)S(1)} %collective-permute-done.10.refs_2_) | copy-start | bytes 491524
  68.0 13.8 %collective-permute-start.14 = (f32[16,128]{1,0:T(8,128)}, f32[16,128]{1,0:T(8,128)S(1)}, u32[]{:S(2)}, u32[]{:S(2)}) collective-permute-start(f32[16,128]{1,0:T(8,128)} %get-tuple-element.13), channel_id=1, source_target_pairs={{0,8},{8,0},{16,24},{24,16},{1,9},{9,1},{17,25},{25,17},{2,10},{10... | collective-permute-start | bytes 24584 | tf_op jit(solution)/shard_map/ppermute | solution.py:273
  70.5 13.6 %collective-permute-start.18 = (f32[16,128]{1,0:T(8,128)}, f32[16,128]{1,0:T(8,128)S(1)}, u32[]{:S(2)}, u32[]{:S(2)}) collective-permute-start(f32[16,128]{1,0:T(8,128)} %get-tuple-element.15), channel_id=1, source_target_pairs={{0,1},{1,0},{2,3},{3,2},{4,5},{5,4},{6,7},{7,6},{8,9},{9,8},{10,11... | collective-permute-start | bytes 24584 | tf_op jit(solution)/shard_map/ppermute | solution.py:273
  72.1 3.9 %collective-permute-start.16 = (f32[16,16]{1,0:T(8,128)}, f32[16,16]{1,0:T(8,128)S(1)}, u32[]{:S(2)}, u32[]{:S(2)}) collective-permute-start(f32[16,16]{1,0:T(8,128)} %get-tuple-element.14), channel_id=1, source_target_pairs={{0,2},{2,0},{4,6},{6,4},{1,3},{3,1},{5,7},{7,5},{8,10},{10,8},{12,... | collective-permute-start | bytes 3080 | tf_op jit(solution)/shard_map/ppermute | solution.py:273
  76.6 4.5 %collective-permute-start.17 = (f32[16,16]{1,0:T(8,128)S(1)}, f32[16,16]{1,0:T(8,128)S(1)}, u32[]{:S(2)}, u32[]{:S(2)}) collective-permute-start(f32[16,16]{1,0:T(8,128)S(1)} %max.18), channel_id=1, source_target_pairs={{0,4},{2,6},{4,0},{6,2},{1,5},{3,7},{5,1},{7,3},{8,12},{10,14},{12... | collective-permute-start | bytes 3080 | tf_op jit(solution)/shard_map/ppermute | solution.py:273
  82.5 3.7 %collective-permute-start.15 = (f32[16,128]{1,0:T(8,128)S(1)}, f32[16,128]{1,0:T(8,128)S(1)}, u32[]{:S(2)}, u32[]{:S(2)}) collective-permute-start(f32[16,128]{1,0:T(8,128)S(1)} %max.16), channel_id=1, source_target_pairs={{0,16},{8,24},{16,0},{24,8},{1,17},{9,25},{17,1},{25,9},{2,18},{10... | collective-permute-start | bytes 24584 | tf_op jit(solution)/shard_map/ppermute | solution.py:273
  (7 other events, 5.7 us)

commit v3 on v2

--- a/solution.py
+++ b/solution.py
@@ -10,7 +10,8 @@
 
 F32 = jnp.float32
 BF16 = jnp.bfloat16
-UNROLL = 8
+UNROLL = 4
+WIDE = 4
 
 
 def split(value):
@@ -96,16 +97,16 @@
 
 def transform_x(s1, s2, table, count_z, count_x, length_x, lanes):
     def step(i, carry):
-        z = i * 2
-        data = jnp.concatenate(
-            [pair_x(s1, (z + j) * count_x, count_x, lanes) for j in range(2)], axis=1
+        z = i * WIDE
+        data = jnp.concatenate(
+            [pair_x(s1, (z + j) * count_x, count_x, lanes) for j in range(WIDE)], axis=1
         )
         out = table_dot(table, data)
-        for j in range(2):
+        for j in range(WIDE):
             s2[pl.ds((z + j) * 2 * length_x, 2 * length_x), :] = out[:, j * lanes : (j + 1) * lanes]
         return carry
 
-    lax.fori_loop(0, count_z // 2, step, 0, unroll=UNROLL)
+    lax.fori_loop(0, count_z // WIDE, step, 0, unroll=UNROLL)
 
 
 def spectrum_body(psf, ty_h, ty_l, fx, fz, spec, s1, s2, *, extent, dims, lanes):
@@ -124,18 +125,18 @@
     table = fx[...]
 
     def step(i, carry):
-        q = i * 2
-        data = jnp.concatenate(
-            [pair_strided(s2, q + j, length_z, extent, 2 * length_z) for j in range(2)], axis=1
+        q = i * WIDE
+        data = jnp.concatenate(
+            [pair_strided(s2, q + j, length_z, extent, 2 * length_z) for j in range(WIDE)], axis=1
         )
         out = table_dot(table, data)
-        for j in range(2):
+        for j in range(WIDE):
             part = out[:, j * lanes : (j + 1) * lanes]
             spec[pl.ds(q + j, length_x, stride=2 * length_z), :] = part[:length_x]
             spec[pl.ds(length_z + q + j, length_x, stride=2 * length_z), :] = part[length_x:]
         return carry
 
-    lax.fori_loop(0, length_z // 2, step, 0, unroll=UNROLL)
+    lax.fori_loop(0, length_z // WIDE, step, 0, unroll=UNROLL)
 
 
 def conv_body(*refs, brick, dims, lanes, groups, parts, conj):
@@ -170,13 +171,13 @@
     back_z = gz[...]
 
     def middle(i, carry):
-        k = i * 2
-        data = jnp.concatenate(
-            [pair_strided(s2, k + j, length_x, wide_z, 2 * length_x) for j in range(2)], axis=1
+        k = i * WIDE
+        data = jnp.concatenate(
+            [pair_strided(s2, k + j, length_x, wide_z, 2 * length_x) for j in range(WIDE)], axis=1
         )
         out = table_dot(forward_z, data)
         kern = jnp.concatenate(
-            [spec[pl.ds((k + j) * 2 * length_z, 2 * length_z), :] for j in range(2)], axis=1
+            [spec[pl.ds((k + j) * 2 * length_z, 2 * length_z), :] for j in range(WIDE)], axis=1
         )
         re, im = out[:length_z], out[length_z:]
         kr, ki = kern[:length_z], kern[length_z:]
@@ -185,18 +186,18 @@
         else:
             prod = jnp.concatenate([re * kr - im * ki, re * ki + im * kr], axis=0)
         back = table_dot(back_z, prod)
-        for j in range(2):
+        for j in range(WIDE):
             s3[pl.ds((k + j) * 2 * brick_z, 2 * brick_z), :] = back[:, j * lanes : (j + 1) * lanes]
         return carry
 
-    lax.fori_loop(0, length_x // 2, middle, 0, unroll=UNROLL)
+    lax.fori_loop(0, length_x // WIDE, middle, 0, unroll=UNROLL)
     back_x = gx[...]
-    for z in range(0, brick_z, 2):
-        data = jnp.concatenate(
-            [pair_strided(s3, z + j, brick_z, length_x, 2 * brick_z) for j in range(2)], axis=1
+    for z in range(0, brick_z, WIDE):
+        data = jnp.concatenate(
+            [pair_strided(s3, z + j, brick_z, length_x, 2 * brick_z) for j in range(WIDE)], axis=1
         )
         out = table_dot(back_x, data)
-        for j in range(2):
+        for j in range(WIDE):
             part = out[:, j * lanes : (j + 1) * lanes]
             s4[pl.ds((z + j) * brick_x, brick_x), :lanes] = part[:brick_x]
             s4[pl.ds((z + j) * brick_x, brick_x), lanes:] = part[brick_x:]

time: 87.2 us -> 83.3 us (0.955)
  Pallas kernels: 31.1 us -> 27.3 us
    pallas_call x2, Pallas kernels: 23 us -> 19.2 us  [convolve(): pl.pallas_call(functools.partial(conv_body, brick=brick, dims=dims, lanes...]
  transfers between devices with their start and end apart: 19 -> 19, of which waited for: 8 -> 8; matrix products, arithmetic and copies ran while one was open for 4% -> 4% of each run, Pallas kernels for 7% -> 8%
where the time goes in v3:
time: 83.3 us; the launch traced here: 82.9 us
  starting transfers between devices  36.2 us (43%)
  Pallas kernels  27.3 us (33%)
  waiting for transfers between devices  11.3 us (14%)
  other arithmetic  5.83 us (7%)
  local copies, waits for them, and re-layouts  1.47 us (2%)
  between operations  0.86 us (1%)
    ppermute x14, starting transfers between devices, swaps(): found.append(lax.ppermute(value, axis, pairs + [(j, i) for i, j in pairs]))  25.4 us
    pallas_call x2, Pallas kernels, convolve(): pl.pallas_call(functools.partial(conv_body, brick=brick, dims=dims, lanes...  19.2 us
    ppermute x5, starting transfers between devices, all_max(): moved.append(lax.ppermute(value, axis, pairs))  10.7 us
    ppermute x14, waiting for transfers between devices, swaps(): found.append(lax.ppermute(value, axis, pairs + [(j, i) for i, j in pairs]))  7.2 us
    pallas_call x1, Pallas kernels, shards(): pl.pallas_call(functools.partial(spectrum_body, extent=extent, dims=dims,...  6.5 us
    ppermute x5, waiting for transfers between devices, all_max(): moved.append(lax.ppermute(value, axis, pairs))  4.07 us
    max x5, other arithmetic, all_max(): jnp.maximum(value, new)  3.97 us
    concatenate x2, other arithmetic, surround(): block = jnp.concatenate([value, halo], axis=0)  1.84 us
  transfers between devices with their start and end apart: 19, of which 8 were waited for; matrix products, arithmetic and copies ran while one was open for 4% of the time, Pallas kernels for 8%

profile of v3, /device:TPU:0, one launch (start us, length us, event | category | flops | bytes accessed | tf_op | source)
XLA Modules:
  0.0 82.9 jit_solution(18369866284112224310)
XLA Ops:
  0.6 1.6 %shard_map.174 = f32[64,128]{1,0:T(8,128)} custom-call(f32[256,128]{1,0:T(8,128)} %bitcast.3), custom_call_target="tpu_custom_call" | custom-call | tf_op jit(solution)/shard_map/pallas_call | solution.py:325
  2.9 5.9 %collective-permute-start = (f32[64,128]{1,0:T(8,128)}, f32[64,128]{1,0:T(8,128)S(1)}, u32[]{:S(2)}, u32[]{:S(2)}) collective-permute-start(f32[64,128]{1,0:T(8,128)} %shard_map.174), channel_id=1, source_target_pairs={{0,2},{4,6},{2,0},{6,4},{1,3},{5,7},{3,1},{7,5},{8,10},{12,14},{10... | collective-permute-start | bytes 98312 | tf_op jit(solution)/shard_map/ppermute | solution.py:239
  8.9 2.1 %collective-permute-done = f32[64,128]{1,0:T(8,128)S(1)} collective-permute-done((f32[64,128]{1,0:T(8,128)}, f32[64,128]{1,0:T(8,128)S(1)}, u32[]{:S(2)}, u32[]{:S(2)}) %collective-permute-start) | collective-permute-done | bytes 32800 | tf_op jit(solution)/shard_map/ppermute | solution.py:239
  11.9 1.6 %collective-permute-start.4 = (f32[320,128]{1,0:T(8,128)S(1)}, f32[320,128]{1,0:T(8,128)S(1)}, u32[]{:S(2)}, u32[]{:S(2)}) collective-permute-start(f32[320,128]{1,0:T(8,128)S(1)} %pad_maximum_fusion.refs_0_), channel_id=1, source_target_pairs={{0,1},{1,0},{2,3},{3,2},{4,5},{5,4},{6,7},{7,6},{8,9},{9,8},{10,11... | collective-permute-start | bytes 491528 | tf_op jit(solution)/shard_map/ppermute | solution.py:239
  14.1 2.9 %collective-permute-start.2 = (f32[320,128]{1,0:T(8,128)S(1)}, f32[320,128]{1,0:T(8,128)S(1)}, u32[]{:S(2)}, u32[]{:S(2)}) collective-permute-start(f32[320,128]{1,0:T(8,128)S(1)} %pad_maximum_fusion.refs_0_), channel_id=1, source_target_pairs={{0,8},{16,24},{8,0},{24,16},{1,9},{17,25},{9,1},{25,17},{2,10},{18... | collective-permute-start | bytes 491528 | tf_op jit(solution)/shard_map/ppermute | solution.py:239
  17.9 2.9 %collective-permute-start.5 = (f32[320,128]{1,0:T(8,128)S(1)}, f32[320,128]{1,0:T(8,128)S(1)}, u32[]{:S(2)}, u32[]{:S(2)}) collective-permute-start(f32[320,128]{1,0:T(8,128)S(1)} %collective-permute-done.4.refs_3_), channel_id=1, source_target_pairs={{0,8},{16,24},{8,0},{24,16},{1,9},{17,25},{9,1},{25,17},{2,10},{18... | collective-permute-start | bytes 491528 | tf_op jit(solution)/shard_map/ppermute | solution.py:239
  20.9 6.5 %shard_map.175.refs_7_ = f32[4608,128]{1,0:T(8,128)} custom-call(f32[32,1024]{1,0:T(8,128)} %psf.1, bf16[4,128,256]{2,1,0:T(8,128)(2,1)} %constant.76.clone.ty_h, bf16[4,128,256]{2,1,0:T(8,128)(2,1)} %constant.77.clone.ty_l, bf16[192,64]{1,0:T(8,128)(2,1)} %constant.78.clone.fx.fz, bf16[192,64]{1,0:T(8,128)(2,1)} %constant.78.clone.fx.fz), custom_call_target="tpu_custom_call" | custom-call | tf_op jit(solution)/shard_map/pallas_call | solution.py:328
  28.2 9.6 %shard_map.176 = (f32[256,128]{1,0:T(8,128)}, f32[64,128]{1,0:T(8,128)}) custom-call(f32[320,128]{1,0:T(8,128)} %copy-done.1, f32[320,128]{1,0:T(8,128)} %copy-done.7, f32[320,128]{1,0:T(8,128)} %copy-done.6, f32[320,128]{1,0:T(8,128)} %copy-done.4, f32[320,128]{1,0:T(8,128)} %copy-done.11, f32[320,128]{1,0:T(8,128)} %copy-done.10, f32[256,128]{1,0:T(8,128)} %bitcast.6, ...), custom_call_target="tpu_custom_call" | custom-call | tf_op jit(solution)/shard_map/pallas_call | solution.py:335
  38.5 3.8 %collective-permute-start.7 = (f32[64,128]{1,0:T(8,128)}, f32[64,128]{1,0:T(8,128)S(1)}, u32[]{:S(2)}, u32[]{:S(2)}) collective-permute-start(f32[64,128]{1,0:T(8,128)} %get-tuple-element.11), channel_id=1, source_target_pairs={{0,2},{4,6},{2,0},{6,4},{1,3},{5,7},{3,1},{7,5},{8,10},{12,14},{10... | collective-permute-start | bytes 98312 | tf_op jit(solution)/shard_map/ppermute | solution.py:239
  42.3 2.1 %collective-permute-done.7 = f32[64,128]{1,0:T(8,128)S(1)} collective-permute-done((f32[64,128]{1,0:T(8,128)}, f32[64,128]{1,0:T(8,128)S(1)}, u32[]{:S(2)}, u32[]{:S(2)}) %collective-permute-start.7) | collective-permute-done | bytes 32800 | tf_op jit(solution)/shard_map/ppermute | solution.py:239
  45.3 1.6 %collective-permute-start.11 = (f32[320,128]{1,0:T(8,128)S(1)}, f32[320,128]{1,0:T(8,128)S(1)}, u32[]{:S(2)}, u32[]{:S(2)}) collective-permute-start(f32[320,128]{1,0:T(8,128)S(1)} %pad_maximum_fusion.1.refs_0_), channel_id=1, source_target_pairs={{0,1},{1,0},{2,3},{3,2},{4,5},{5,4},{6,7},{7,6},{8,9},{9,8},{10,11... | collective-permute-start | bytes 491528 | tf_op jit(solution)/shard_map/ppermute | solution.py:239
  47.6 1.3 %collective-permute-start.9 = (f32[320,128]{1,0:T(8,128)S(1)}, f32[320,128]{1,0:T(8,128)S(1)}, u32[]{:S(2)}, u32[]{:S(2)}) collective-permute-start(f32[320,128]{1,0:T(8,128)S(1)} %pad_maximum_fusion.1.refs_0_), channel_id=1, source_target_pairs={{0,8},{16,24},{8,0},{24,16},{1,9},{17,25},{9,1},{25,17},{2,10},{18... | collective-permute-start | bytes 491528 | tf_op jit(solution)/shard_map/ppermute | solution.py:239
  48.9 1.8 %collective-permute-done.11.refs_3_ = f32[320,128]{1,0:T(8,128)S(1)} collective-permute-done((f32[320,128]{1,0:T(8,128)S(1)}, f32[320,128]{1,0:T(8,128)S(1)}, u32[]{:S(2)}, u32[]{:S(2)}) %collective-permute-start.11) | collective-permute-done | bytes 163872 | tf_op jit(solution)/shard_map/ppermute | solution.py:239
  51.4 1.5 %collective-permute-start.12 = (f32[320,128]{1,0:T(8,128)S(1)}, f32[320,128]{1,0:T(8,128)S(1)}, u32[]{:S(2)}, u32[]{:S(2)}) collective-permute-start(f32[320,128]{1,0:T(8,128)S(1)} %collective-permute-done.11.refs_3_), channel_id=1, source_target_pairs={{0,8},{16,24},{8,0},{24,16},{1,9},{17,25},{9,1},{25,17},{2,10},{18... | collective-permute-start | bytes 491528 | tf_op jit(solution)/shard_map/ppermute | solution.py:239
  52.9 1.0 %collective-permute-done.12.refs_4_ = f32[320,128]{1,0:T(8,128)S(1)} collective-permute-done((f32[320,128]{1,0:T(8,128)S(1)}, f32[320,128]{1,0:T(8,128)S(1)}, u32[]{:S(2)}, u32[]{:S(2)}) %collective-permute-start.12) | collective-permute-done | bytes 163872 | tf_op jit(solution)/shard_map/ppermute | solution.py:239
  54.5 9.6 %shard_map.177 = (f32[256,128]{1,0:T(8,128)}, f32[16,128]{1,0:T(8,128)}, f32[16,128]{1,0:T(8,128)}, f32[16,16]{1,0:T(8,128)}) custom-call(f32[320,128]{1,0:T(8,128)} %copy-done, f32[320,128]{1,0:T(8,128)} %copy-done.5, f32[320,128]{1,0:T(8,128)} %copy-done.3, f32[320,128]{1,0:T(8,128)} %copy-done.2, f32[320,128]{1,0:T(8,128)} %copy-done.9, ...), custom_call_target="tpu_custom_call" | custom-call | tf_op jit(solution)/shard_map/pallas_call | solution.py:335
  64.1 2.6 %collective-permute-start.14 = (f32[16,128]{1,0:T(8,128)}, f32[16,128]{1,0:T(8,128)S(1)}, u32[]{:S(2)}, u32[]{:S(2)}) collective-permute-start(f32[16,128]{1,0:T(8,128)} %get-tuple-element.13), channel_id=1, source_target_pairs={{0,8},{8,0},{16,24},{24,16},{1,9},{9,1},{17,25},{25,17},{2,10},{10... | collective-permute-start | bytes 24584 | tf_op jit(solution)/shard_map/ppermute | solution.py:274
  66.7 1.5 %collective-permute-start.18 = (f32[16,128]{1,0:T(8,128)}, f32[16,128]{1,0:T(8,128)S(1)}, u32[]{:S(2)}, u32[]{:S(2)}) collective-permute-start(f32[16,128]{1,0:T(8,128)} %get-tuple-element.15), channel_id=1, source_target_pairs={{0,1},{1,0},{2,3},{3,2},{4,5},{5,4},{6,7},{7,6},{8,9},{9,8},{10,11... | collective-permute-start | bytes 24584 | tf_op jit(solution)/shard_map/ppermute | solution.py:274
  68.2 2.0 %collective-permute-start.16 = (f32[16,16]{1,0:T(8,128)}, f32[16,16]{1,0:T(8,128)S(1)}, u32[]{:S(2)}, u32[]{:S(2)}) collective-permute-start(f32[16,16]{1,0:T(8,128)} %get-tuple-element.14), channel_id=1, source_target_pairs={{0,2},{2,0},{4,6},{6,4},{1,3},{3,1},{5,7},{7,5},{8,10},{10,8},{12,... | collective-permute-start | bytes 3080 | tf_op jit(solution)/shard_map/ppermute | solution.py:274
  70.2 1.8 %collective-permute-done.16 = f32[16,16]{1,0:T(8,128)S(1)} collective-permute-done((f32[16,16]{1,0:T(8,128)}, f32[16,16]{1,0:T(8,128)S(1)}, u32[]{:S(2)}, u32[]{:S(2)}) %collective-permute-start.16) | collective-permute-done | bytes 1056 | tf_op jit(solution)/shard_map/ppermute | solution.py:274
  72.8 2.9 %collective-permute-start.17 = (f32[16,16]{1,0:T(8,128)S(1)}, f32[16,16]{1,0:T(8,128)S(1)}, u32[]{:S(2)}, u32[]{:S(2)}) collective-permute-start(f32[16,16]{1,0:T(8,128)S(1)} %max.18), channel_id=1, source_target_pairs={{0,4},{2,6},{4,0},{6,2},{1,5},{3,7},{5,1},{7,3},{8,12},{10,14},{12... | collective-permute-start | bytes 3080 | tf_op jit(solution)/shard_map/ppermute | solution.py:274
  75.7 1.6 %collective-permute-done.17 = f32[16,16]{1,0:T(8,128)S(1)} collective-permute-done((f32[16,16]{1,0:T(8,128)S(1)}, f32[16,16]{1,0:T(8,128)S(1)}, u32[]{:S(2)}, u32[]{:S(2)}) %collective-permute-start.17) | collective-permute-done | bytes 1056 | tf_op jit(solution)/shard_map/ppermute | solution.py:274
  78.6 1.7 %collective-permute-start.15 = (f32[16,128]{1,0:T(8,128)S(1)}, f32[16,128]{1,0:T(8,128)S(1)}, u32[]{:S(2)}, u32[]{:S(2)}) collective-permute-start(f32[16,128]{1,0:T(8,128)S(1)} %max.16), channel_id=1, source_target_pairs={{0,16},{8,24},{16,0},{24,8},{1,17},{9,25},{17,1},{25,9},{2,18},{10... | collective-permute-start | bytes 24584 | tf_op jit(solution)/shard_map/ppermute | solution.py:274
  80.3 1.4 %dynamic-slice_maximum_fusion = f32[16,64]{1,0:T(8,128)} fusion(f32[16,128]{1,0:T(8,128)S(1)} %collective-permute-done.18, s32[]{:T(128)S(6)} %select_n.31, f32[16,128]{1,0:T(8,128)} %get-tuple-element.15), kind=kLoop, calls=%fused_computation.6 | loop fusion | flops 1024 | bytes 12292 | tf_op jit(solution)/shard_map/max | solution.py:277
  (54 shorter events, 10.7 us)
Async XLA Ops:
  2.3 6.6 %collective-permute-start.1 = (f32[64,128]{1,0:T(8,128)}, f32[64,128]{1,0:T(8,128)S(1)}, u32[]{:S(2)}, u32[]{:S(2)}) collective-permute-start(f32[64,128]{1,0:T(8,128)} %shard_map.174), channel_id=1, source_target_pairs={{2,4},{4,2},{3,5},{5,3},{10,12},{12,10},{11,13},{13,11},{18,20},{2... | collective-permute-start | bytes 98312 | tf_op jit(solution)/shard_map/ppermute | solution.py:239
  2.9 8.0 %collective-permute-start = (f32[64,128]{1,0:T(8,128)}, f32[64,128]{1,0:T(8,128)S(1)}, u32[]{:S(2)}, u32[]{:S(2)}) collective-permute-start(f32[64,128]{1,0:T(8,128)} %shard_map.174), channel_id=1, source_target_pairs={{0,2},{4,6},{2,0},{6,4},{1,3},{5,7},{3,1},{7,5},{8,10},{12,14},{10... | collective-permute-start | bytes 98312 | tf_op jit(solution)/shard_map/ppermute | solution.py:239
  11.9 15.5 %copy-start.1 = (f32[320,128]{1,0:T(8,128)}, f32[320,128]{1,0:T(8,128)S(1)}, u32[]{:S(2)}) copy-start(f32[320,128]{1,0:T(8,128)S(1)} %pad_maximum_fusion.refs_0_) | copy-start | bytes 491524
  11.9 5.4 %collective-permute-start.4 = (f32[320,128]{1,0:T(8,128)S(1)}, f32[320,128]{1,0:T(8,128)S(1)}, u32[]{:S(2)}, u32[]{:S(2)}) collective-permute-start(f32[320,128]{1,0:T(8,128)S(1)} %pad_maximum_fusion.refs_0_), channel_id=1, source_target_pairs={{0,1},{1,0},{2,3},{3,2},{4,5},{5,4},{6,7},{7,6},{8,9},{9,8},{10,11... | collective-permute-start | bytes 491528 | tf_op jit(solution)/shard_map/ppermute | solution.py:239
  13.5 13.9 %collective-permute-start.3 = (f32[320,128]{1,0:T(8,128)S(1)}, f32[320,128]{1,0:T(8,128)S(1)}, u32[]{:S(2)}, u32[]{:S(2)}) collective-permute-start(f32[320,128]{1,0:T(8,128)S(1)} %pad_maximum_fusion.refs_0_), channel_id=1, source_target_pairs={{8,16},{16,8},{9,17},{17,9},{10,18},{18,10},{11,19},{19,11},{12,20... | collective-permute-start | bytes 491528 | tf_op jit(solution)/shard_map/ppermute | solution.py:239
  14.1 13.2 %collective-permute-start.2 = (f32[320,128]{1,0:T(8,128)S(1)}, f32[320,128]{1,0:T(8,128)S(1)}, u32[]{:S(2)}, u32[]{:S(2)}) collective-permute-start(f32[320,128]{1,0:T(8,128)S(1)} %pad_maximum_fusion.refs_0_), channel_id=1, source_target_pairs={{0,8},{16,24},{8,0},{24,16},{1,9},{17,25},{9,1},{25,17},{2,10},{18... | collective-permute-start | bytes 491528 | tf_op jit(solution)/shard_map/ppermute | solution.py:239
  17.3 10.2 %copy-start.4 = (f32[320,128]{1,0:T(8,128)}, f32[320,128]{1,0:T(8,128)S(1)}, u32[]{:S(2)}) copy-start(f32[320,128]{1,0:T(8,128)S(1)} %collective-permute-done.4.refs_3_) | copy-start | bytes 491524
  17.3 10.1 %collective-permute-start.6 = (f32[320,128]{1,0:T(8,128)S(1)}, f32[320,128]{1,0:T(8,128)S(1)}, u32[]{:S(2)}, u32[]{:S(2)}) collective-permute-start(f32[320,128]{1,0:T(8,128)S(1)} %collective-permute-done.4.refs_3_), channel_id=1, source_target_pairs={{8,16},{16,8},{9,17},{17,9},{10,18},{18,10},{11,19},{19,11},{12,20... | collective-permute-start | bytes 491528 | tf_op jit(solution)/shard_map/ppermute | solution.py:239
  17.9 9.5 %collective-permute-start.5 = (f32[320,128]{1,0:T(8,128)S(1)}, f32[320,128]{1,0:T(8,128)S(1)}, u32[]{:S(2)}, u32[]{:S(2)}) collective-permute-start(f32[320,128]{1,0:T(8,128)S(1)} %collective-permute-done.4.refs_3_), channel_id=1, source_target_pairs={{0,8},{16,24},{8,0},{24,16},{1,9},{17,25},{9,1},{25,17},{2,10},{18... | collective-permute-start | bytes 491528 | tf_op jit(solution)/shard_map/ppermute | solution.py:239
  37.8 4.4 %collective-permute-start.8 = (f32[64,128]{1,0:T(8,128)}, f32[64,128]{1,0:T(8,128)S(1)}, u32[]{:S(2)}, u32[]{:S(2)}) collective-permute-start(f32[64,128]{1,0:T(8,128)} %get-tuple-element.11), channel_id=1, source_target_pairs={{2,4},{4,2},{3,5},{5,3},{10,12},{12,10},{11,13},{13,11},{18,20},{2... | collective-permute-start | bytes 98312 | tf_op jit(solution)/shard_map/ppermute | solution.py:239
  38.5 5.9 %collective-permute-start.7 = (f32[64,128]{1,0:T(8,128)}, f32[64,128]{1,0:T(8,128)S(1)}, u32[]{:S(2)}, u32[]{:S(2)}) collective-permute-start(f32[64,128]{1,0:T(8,128)} %get-tuple-element.11), channel_id=1, source_target_pairs={{0,2},{4,6},{2,0},{6,4},{1,3},{5,7},{3,1},{7,5},{8,10},{12,14},{10... | collective-permute-start | bytes 98312 | tf_op jit(solution)/shard_map/ppermute | solution.py:239
  45.3 8.6 %copy-start = (f32[320,128]{1,0:T(8,128)}, f32[320,128]{1,0:T(8,128)S(1)}, u32[]{:S(2)}) copy-start(f32[320,128]{1,0:T(8,128)S(1)} %pad_maximum_fusion.1.refs_0_) | copy-start | bytes 491524
  45.3 5.4 %collective-permute-start.11 = (f32[320,128]{1,0:T(8,128)S(1)}, f32[320,128]{1,0:T(8,128)S(1)}, u32[]{:S(2)}, u32[]{:S(2)}) collective-permute-start(f32[320,128]{1,0:T(8,128)S(1)} %pad_maximum_fusion.1.refs_0_), channel_id=1, source_target_pairs={{0,1},{1,0},{2,3},{3,2},{4,5},{5,4},{6,7},{7,6},{8,9},{9,8},{10,11... | collective-permute-start | bytes 491528 | tf_op jit(solution)/shard_map/ppermute | solution.py:239
  46.9 5.9 %collective-permute-start.10 = (f32[320,128]{1,0:T(8,128)S(1)}, f32[320,128]{1,0:T(8,128)S(1)}, u32[]{:S(2)}, u32[]{:S(2)}) collective-permute-start(f32[320,128]{1,0:T(8,128)S(1)} %pad_maximum_fusion.1.refs_0_), channel_id=1, source_target_pairs={{8,16},{16,8},{9,17},{17,9},{10,18},{18,10},{11,19},{19,11},{12,20... | collective-permute-start | bytes 491528 | tf_op jit(solution)/shard_map/ppermute | solution.py:239
  47.6 5.3 %collective-permute-start.9 = (f32[320,128]{1,0:T(8,128)S(1)}, f32[320,128]{1,0:T(8,128)S(1)}, u32[]{:S(2)}, u32[]{:S(2)}) collective-permute-start(f32[320,128]{1,0:T(8,128)S(1)} %pad_maximum_fusion.1.refs_0_), channel_id=1, source_target_pairs={{0,8},{16,24},{8,0},{24,16},{1,9},{17,25},{9,1},{25,17},{2,10},{18... | collective-permute-start | bytes 491528 | tf_op jit(solution)/shard_map/ppermute | solution.py:239
  50.7 3.2 %copy-start.2 = (f32[320,128]{1,0:T(8,128)}, f32[320,128]{1,0:T(8,128)S(1)}, u32[]{:S(2)}) copy-start(f32[320,128]{1,0:T(8,128)S(1)} %collective-permute-done.11.refs_3_) | copy-start | bytes 491524
  50.7 2.2 %collective-permute-start.13 = (f32[320,128]{1,0:T(8,128)S(1)}, f32[320,128]{1,0:T(8,128)S(1)}, u32[]{:S(2)}, u32[]{:S(2)}) collective-permute-start(f32[320,128]{1,0:T(8,128)S(1)} %collective-permute-done.11.refs_3_), channel_id=1, source_target_pairs={{8,16},{16,8},{9,17},{17,9},{10,18},{18,10},{11,19},{19,11},{12,20... | collective-permute-start | bytes 491528 | tf_op jit(solution)/shard_map/ppermute | solution.py:239
  51.4 2.5 %collective-permute-start.12 = (f32[320,128]{1,0:T(8,128)S(1)}, f32[320,128]{1,0:T(8,128)S(1)}, u32[]{:S(2)}, u32[]{:S(2)}) collective-permute-start(f32[320,128]{1,0:T(8,128)S(1)} %collective-permute-done.11.refs_3_), channel_id=1, source_target_pairs={{0,8},{16,24},{8,0},{24,16},{1,9},{17,25},{9,1},{25,17},{2,10},{18... | collective-permute-start | bytes 491528 | tf_op jit(solution)/shard_map/ppermute | solution.py:239
  52.8 1.0 %copy-start.3 = (f32[320,128]{1,0:T(8,128)}, f32[320,128]{1,0:T(8,128)S(1)}, u32[]{:S(2)}) copy-start(f32[320,128]{1,0:T(8,128)S(1)} %collective-permute-done.10.refs_2_) | copy-start | bytes 491524
  64.1 13.8 %collective-permute-start.14 = (f32[16,128]{1,0:T(8,128)}, f32[16,128]{1,0:T(8,128)S(1)}, u32[]{:S(2)}, u32[]{:S(2)}) collective-permute-start(f32[16,128]{1,0:T(8,128)} %get-tuple-element.13), channel_id=1, source_target_pairs={{0,8},{8,0},{16,24},{24,16},{1,9},{9,1},{17,25},{25,17},{2,10},{10... | collective-permute-start | bytes 24584 | tf_op jit(solution)/shard_map/ppermute | solution.py:274
  66.7 13.6 %collective-permute-start.18 = (f32[16,128]{1,0:T(8,128)}, f32[16,128]{1,0:T(8,128)S(1)}, u32[]{:S(2)}, u32[]{:S(2)}) collective-permute-start(f32[16,128]{1,0:T(8,128)} %get-tuple-element.15), channel_id=1, source_target_pairs={{0,1},{1,0},{2,3},{3,2},{4,5},{5,4},{6,7},{7,6},{8,9},{9,8},{10,11... | collective-permute-start | bytes 24584 | tf_op jit(solution)/shard_map/ppermute | solution.py:274
  68.2 3.9 %collective-permute-start.16 = (f32[16,16]{1,0:T(8,128)}, f32[16,16]{1,0:T(8,128)S(1)}, u32[]{:S(2)}, u32[]{:S(2)}) collective-permute-start(f32[16,16]{1,0:T(8,128)} %get-tuple-element.14), channel_id=1, source_target_pairs={{0,2},{2,0},{4,6},{6,4},{1,3},{3,1},{5,7},{7,5},{8,10},{10,8},{12,... | collective-permute-start | bytes 3080 | tf_op jit(solution)/shard_map/ppermute | solution.py:274
  72.8 4.5 %collective-permute-start.17 = (f32[16,16]{1,0:T(8,128)S(1)}, f32[16,16]{1,0:T(8,128)S(1)}, u32[]{:S(2)}, u32[]{:S(2)}) collective-permute-start(f32[16,16]{1,0:T(8,128)S(1)} %max.18), channel_id=1, source_target_pairs={{0,4},{2,6},{4,0},{6,2},{1,5},{3,7},{5,1},{7,3},{8,12},{10,14},{12... | collective-permute-start | bytes 3080 | tf_op jit(solution)/shard_map/ppermute | solution.py:274
  78.6 3.7 %collective-permute-start.15 = (f32[16,128]{1,0:T(8,128)S(1)}, f32[16,128]{1,0:T(8,128)S(1)}, u32[]{:S(2)}, u32[]{:S(2)}) collective-permute-start(f32[16,128]{1,0:T(8,128)S(1)} %max.16), channel_id=1, source_target_pairs={{0,16},{8,24},{16,0},{24,8},{1,17},{9,25},{17,1},{25,9},{2,18},{10... | collective-permute-start | bytes 24584 | tf_op jit(solution)/shard_map/ppermute | solution.py:274
  (7 other events, 5.7 us)
